TPU v7x, 8 devices: a whole 2x2x1 slice. The times are simulated.
8 devices in a mesh: data: 1 (over z), inner: 2 (over y), stage: 4 (over x, core).
Axes of the slice: x: 2, y: 2, z: 1, core: 2. Of those that a mesh axis runs over, the one named last changes fastest.
Arguments:
- x_tokens: bfloat16 [16, 32, 2048], P(('data', 'stage', 'inner'))
- g_cotan: bfloat16 [16, 32, 2048], P(('data', 'stage', 'inner'))
- w_up: bfloat16 [1, 4, 2048, 8192], P(None, ('data', 'stage'), None, 'inner')
- w_down: bfloat16 [1, 4, 8192, 2048], P(None, ('data', 'stage'), 'inner')
Outputs:
- output 1: bfloat16 [16, 32, 2048], P(('data', 'stage', 'inner'))
- output 2: bfloat16 [16, 32, 2048], P(('data', 'stage', 'inner'))
- output 3: float32 [1, 4, 2048, 8192], P(None, ('data', 'stage'), None, 'inner')
- output 4: float32 [1, 4, 8192, 2048], P(None, ('data', 'stage'), 'inner')
All inputs are finite; a program needn't handle non-finite values.
Results may differ from a plain program's by a relative error of at most 0.0124555.
Values are sent between devices in bfloat16 or wider.
A program may use at most 1 GiB of HBM per device.

v0:
```python
import jax
import jax.numpy as jnp
from jax import lax
from jax.sharding import PartitionSpec as P


def gelu_pair(pre_act):
    normal_cdf = 0.5 * (1.0 + lax.erf(pre_act * 0.7071067811865476))
    normal_pdf = jnp.exp(-0.5 * pre_act * pre_act) * 0.3989422804014327
    return pre_act * normal_cdf, normal_cdf + pre_act * normal_pdf


def layer_fwd(h_in, w_one, w_two):
    pre_act = jnp.dot(h_in, w_one, preferred_element_type=jnp.float32)
    act_val = gelu_pair(pre_act)[0].astype(jnp.bfloat16)
    branch = jnp.dot(act_val, w_two, preferred_element_type=jnp.float32)
    return (h_in.astype(jnp.float32) + branch).astype(jnp.bfloat16)


def layer_bwd(h_in, w_one, w_two, g_out):
    pre_act = jnp.dot(h_in, w_one, preferred_element_type=jnp.float32)
    gelu_val, gelu_grad = gelu_pair(pre_act)
    act_val = gelu_val.astype(jnp.bfloat16)
    d_act = lax.dot_general(g_out, w_two, (((1,), (1,)), ((), ())), preferred_element_type=jnp.float32)
    d_pre = (d_act * gelu_grad).astype(jnp.bfloat16)
    grad_one = lax.dot_general(h_in, d_pre, (((0,), (0,)), ((), ())), preferred_element_type=jnp.float32)
    grad_two = lax.dot_general(act_val, g_out, (((0,), (0,)), ((), ())), preferred_element_type=jnp.float32)
    back_term = lax.dot_general(d_pre, w_one, (((1,), (1,)), ((), ())), preferred_element_type=jnp.float32)
    g_in = (g_out.astype(jnp.float32) + back_term).astype(jnp.bfloat16)
    return g_in, grad_one, grad_two


def solution(mesh):
    n_stage = mesh.shape['stage']
    tok_spec = P(('data', 'stage', 'inner'))
    up_spec = P(None, ('data', 'stage'), None, 'inner')
    down_spec = P(None, ('data', 'stage'), 'inner', None)
    fwd_perm = [(src_idx, (src_idx + 1) % n_stage) for src_idx in range(n_stage)]
    bwd_perm = [(src_idx, (src_idx - 1) % n_stage) for src_idx in range(n_stage)]

    def device_step(x_loc, g_loc, w_up, w_down):
        n_virt = w_up.shape[0]
        group_layers = w_up.shape[1]
        d_model = x_loc.shape[2]
        stage_idx = lax.axis_index('stage')
        is_first = stage_idx == 0
        is_last = stage_idx == n_stage - 1
        x_col = lax.all_gather(x_loc, 'stage', axis=0, tiled=True)
        g_col = lax.all_gather(g_loc, 'stage', axis=0, tiled=True)
        n_micro = x_col.shape[0]
        tick_ids = jnp.arange(n_micro + n_stage - 1)
        act_zero = jnp.zeros(x_loc.shape[1:], x_loc.dtype)
        stash_list = []
        act_buf = x_col
        for virt_idx in range(n_virt):
            up_full = lax.all_gather(w_up[virt_idx], 'inner', axis=2, tiled=True)
            down_full = lax.all_gather(w_down[virt_idx], 'inner', axis=1, tiled=True)

            def fwd_tick(loop_state, tick_idx):
                buf_in, recv_act, saved_ins = loop_state
                micro_idx = tick_idx - stage_idx
                is_valid = (micro_idx >= 0) & (micro_idx < n_micro)
                buf_slot = jnp.clip(micro_idx, 0, n_micro - 1)
                from_buf = lax.dynamic_index_in_dim(buf_in, buf_slot, 0, keepdims=False)
                h_act = jnp.where(is_first, from_buf, recv_act)
                layer_ins = []
                for layer_idx in range(group_layers):
                    layer_ins.append(h_act)
                    h_act = layer_fwd(h_act, up_full[layer_idx], down_full[layer_idx])
                old_ins = lax.dynamic_index_in_dim(saved_ins, buf_slot, 0, keepdims=False)
                new_ins = jnp.where(is_valid, jnp.stack(layer_ins), old_ins)
                saved_ins = lax.dynamic_update_index_in_dim(saved_ins, new_ins, buf_slot, 0)
                sent_act = lax.ppermute(h_act, 'stage', fwd_perm)
                done_idx = tick_idx - (n_stage - 1)
                done_slot = jnp.clip(done_idx, 0, n_micro - 1)
                prev_val = lax.dynamic_index_in_dim(buf_in, done_slot, 0, keepdims=False)
                keep_new = is_first & (done_idx >= 0)
                buf_in = lax.dynamic_update_index_in_dim(buf_in, jnp.where(keep_new, sent_act, prev_val), done_slot, 0)
                return (buf_in, sent_act, saved_ins), None

            saved_init = jnp.zeros((n_micro, group_layers) + x_loc.shape[1:], x_loc.dtype)
            end_state = lax.scan(fwd_tick, (act_buf, act_zero, saved_init), tick_ids)[0]
            act_buf = end_state[0]
            stash_list.append(end_state[2])
        y_src = jnp.where(is_first, act_buf, jnp.zeros_like(act_buf))
        y_loc = lax.psum_scatter(y_src, 'stage', scatter_dimension=0, tiled=True)

        grad_buf = g_col
        up_out = [None] * n_virt
        down_out = [None] * n_virt
        for virt_idx in reversed(range(n_virt)):
            up_full = lax.all_gather(w_up[virt_idx], 'inner', axis=2, tiled=True)
            down_full = lax.all_gather(w_down[virt_idx], 'inner', axis=1, tiled=True)
            d_ff = up_full.shape[2]
            saved_ins = stash_list[virt_idx]

            def bwd_tick(loop_state, tick_idx):
                buf_in, recv_grad, acc_one, acc_two = loop_state
                micro_idx = tick_idx - (n_stage - 1 - stage_idx)
                is_valid = (micro_idx >= 0) & (micro_idx < n_micro)
                buf_slot = jnp.clip(micro_idx, 0, n_micro - 1)
                from_buf = lax.dynamic_index_in_dim(buf_in, buf_slot, 0, keepdims=False)
                g_act = jnp.where(is_last, from_buf, recv_grad)
                g_act = jnp.where(is_valid, g_act, jnp.zeros_like(g_act))
                layer_ins = lax.dynamic_index_in_dim(saved_ins, buf_slot, 0, keepdims=False)
                acc_one = list(acc_one)
                acc_two = list(acc_two)
                for layer_idx in reversed(range(group_layers)):
                    g_act, grad_one, grad_two = layer_bwd(layer_ins[layer_idx], up_full[layer_idx], down_full[layer_idx], g_act)
                    acc_one[layer_idx] = acc_one[layer_idx] + grad_one
                    acc_two[layer_idx] = acc_two[layer_idx] + grad_two
                sent_grad = lax.ppermute(g_act, 'stage', bwd_perm)
                done_idx = tick_idx - (n_stage - 1)
                done_slot = jnp.clip(done_idx, 0, n_micro - 1)
                prev_val = lax.dynamic_index_in_dim(buf_in, done_slot, 0, keepdims=False)
                keep_new = is_last & (done_idx >= 0)
                buf_in = lax.dynamic_update_index_in_dim(buf_in, jnp.where(keep_new, sent_grad, prev_val), done_slot, 0)
                return (buf_in, sent_grad, acc_one, acc_two), None

            acc_init_one = [jnp.zeros((d_model, d_ff), jnp.float32) for layer_idx in range(group_layers)]
            acc_init_two = [jnp.zeros((d_ff, d_model), jnp.float32) for layer_idx in range(group_layers)]
            end_state = lax.scan(bwd_tick, (grad_buf, act_zero, acc_init_one, acc_init_two), tick_ids)[0]
            grad_buf = end_state[0]
            up_out[virt_idx] = lax.psum_scatter(jnp.stack(end_state[2]), 'inner', scatter_dimension=2, tiled=True)
            down_out[virt_idx] = lax.psum_scatter(jnp.stack(end_state[3]), 'inner', scatter_dimension=1, tiled=True)
        dx_src = jnp.where(is_last, grad_buf, jnp.zeros_like(grad_buf))
        dx_loc = lax.psum_scatter(dx_src, 'stage', scatter_dimension=0, tiled=True)
        return y_loc, dx_loc, jnp.stack(up_out), jnp.stack(down_out)

    return jax.shard_map(device_step, mesh=mesh, in_specs=(tok_spec, tok_spec, up_spec, down_spec), out_specs=(tok_spec, tok_spec, up_spec, down_spec), check_vma=False)
```

profile of v0, /device:TPU:0, one launch (start us, length us, event | category | flops | bytes accessed | tf_op | source)
XLA Modules:
  0.0 4191.9 jit_solution(11057112192213031675)
XLA Ops:
  26.1 387.1 %all-gather.11.cloned.1.call-done = bf16[1,1,2048,8192]{3,2,1,0:T(8,128)(2,1)} async-done(((bf16[1,1,2048,4096]{3,2,1,0:T(8,128)(2,1)}), bf16[1,1,2048,8192]{3,2,1,0:T(8,128)(2,1)}) %all-gather.11.cloned.1.call-update) | async-done | bytes 33554448 | tf_op jit(solution)/shard_map/all_gather | solution.py:56
  413.1 387.1 %all-gather.13.cloned.1.call-done = bf16[1,1,8192,2048]{3,2,1,0:T(8,128)(2,1)} async-done(((bf16[1,1,4096,2048]{3,2,1,0:T(8,128)(2,1)}), bf16[1,1,8192,2048]{3,2,1,0:T(8,128)(2,1)}) %all-gather.13.cloned.1.call-update) | async-done | bytes 33554448 | tf_op jit(solution)/shard_map/all_gather | solution.py:57
  800.3 391.8 %while.35 = (s32[]{:T(128)}, bf16[8,32,2048]{2,1,0:T(8,128)(2,1)}, bf16[32,2048]{1,0:T(8,128)(2,1)S(1)}, bf16[8,1,32,2048]{3,2,1,0:T(8,128)(2,1)S(1)}, s32[11]{0...) while((s32[]{:T(128)}, bf16[8,32,2048]{2,1,0:T(8,128)(2,1)}, ...), condition=%wide.region_1.2_spmd, body=%wide.region_0.1_spmd.sunk | while | flops 2149318656 | bytes 69994800 | solution.py:82
  801.7 29.2 fusion.73
  837.3 29.2 fusion.73
  872.9 29.2 fusion.73
  944.1 29.3 fusion.73
  979.8 29.2 fusion.73
  1015.5 29.2 fusion.73
  1194.7 1511.5 %while.36 = (s32[]{:T(128)}, bf16[8,32,2048]{2,1,0:T(8,128)(2,1)}, bf16[32,2048]{1,0:T(8,128)(2,1)S(1)}, f32[2048,8192]{1,0:T(8,128)}, f32[8192,2048]{1,0:T(8,12...) while((s32[]{:T(128)}, bf16[8,32,2048]{2,1,0:T(8,128)(2,1)}, ...), condition=%wide.region_4.5_spmd.clone, body=%wide.region_3.4_spmd.clone.sunk | while | flops 5440143360 | bytes 376176960 | solution.py:122
  1335.7 46.5 %select_add_fusion.5 = f32[8192,2048]{1,0:T(8,128)} fusion(f32[8192,2048]{1,0:T(8,128)} %get-tuple-element.524, bf16[32,2048]{1,0:T(8,128)(2,1)S(1)} %fusion.83, pred[]{:T(512)S(6)} %compare.3, f32[32,8192]{1,0:T(8,128)S(1)} %fusion.84), kind=kOutput, calls=%fused_computation.21.clone.1 | convolution fusion | flops 1108606976 | bytes 135397376 | tf_op jit(solution)/shard_map/while/body/eval_jaxpr/dot_general | solution.py:27
  1382.2 46.5 %select_add_fusion.4 = f32[2048,8192]{1,0:T(8,128)} fusion(f32[2048,8192]{1,0:T(8,128)} %get-tuple-element.523, pred[]{:T(512)S(6)} %compare.3, bf16[32,8192]{1,0:T(8,128)(2,1)S(1)} %fusion.85, bf16[8,1,32,2048]{3,2,1,0:T(8,128)(2,1)S(1)} %get-tuple-element.545, s32[]{:T(128)S(6)} %min.34), kind=kOutput, calls=%fused_computation.22.clone.1 | convolution fusion | flops 1107296256 | bytes 134873088 | tf_op jit(solution)/shard_map/while/body/eval_jaxpr/dot_general | solution.py:26
  1477.0 46.5 %select_add_fusion.5 = f32[8192,2048]{1,0:T(8,128)} fusion(f32[8192,2048]{1,0:T(8,128)} %get-tuple-element.524, bf16[32,2048]{1,0:T(8,128)(2,1)S(1)} %fusion.83, pred[]{:T(512)S(6)} %compare.3, f32[32,8192]{1,0:T(8,128)S(1)} %fusion.84), kind=kOutput, calls=%fused_computation.21.clone.1 | convolution fusion | flops 1108606976 | bytes 135397376 | tf_op jit(solution)/shard_map/while/body/eval_jaxpr/dot_general | solution.py:27
  1523.5 46.5 %select_add_fusion.4 = f32[2048,8192]{1,0:T(8,128)} fusion(f32[2048,8192]{1,0:T(8,128)} %get-tuple-element.523, pred[]{:T(512)S(6)} %compare.3, bf16[32,8192]{1,0:T(8,128)(2,1)S(1)} %fusion.85, bf16[8,1,32,2048]{3,2,1,0:T(8,128)(2,1)S(1)} %get-tuple-element.545, s32[]{:T(128)S(6)} %min.34), kind=kOutput, calls=%fused_computation.22.clone.1 | convolution fusion | flops 1107296256 | bytes 134873088 | tf_op jit(solution)/shard_map/while/body/eval_jaxpr/dot_general | solution.py:26
  1619.9 46.5 %select_add_fusion.5 = f32[8192,2048]{1,0:T(8,128)} fusion(f32[8192,2048]{1,0:T(8,128)} %get-tuple-element.524, bf16[32,2048]{1,0:T(8,128)(2,1)S(1)} %fusion.83, pred[]{:T(512)S(6)} %compare.3, f32[32,8192]{1,0:T(8,128)S(1)} %fusion.84), kind=kOutput, calls=%fused_computation.21.clone.1 | convolution fusion | flops 1108606976 | bytes 135397376 | tf_op jit(solution)/shard_map/while/body/eval_jaxpr/dot_general | solution.py:27
  1666.4 46.5 %select_add_fusion.4 = f32[2048,8192]{1,0:T(8,128)} fusion(f32[2048,8192]{1,0:T(8,128)} %get-tuple-element.523, pred[]{:T(512)S(6)} %compare.3, bf16[32,8192]{1,0:T(8,128)(2,1)S(1)} %fusion.85, bf16[8,1,32,2048]{3,2,1,0:T(8,128)(2,1)S(1)} %get-tuple-element.545, s32[]{:T(128)S(6)} %min.34), kind=kOutput, calls=%fused_computation.22.clone.1 | convolution fusion | flops 1107296256 | bytes 134873088 | tf_op jit(solution)/shard_map/while/body/eval_jaxpr/dot_general | solution.py:26
  1761.2 46.5 %select_add_fusion.5 = f32[8192,2048]{1,0:T(8,128)} fusion(f32[8192,2048]{1,0:T(8,128)} %get-tuple-element.524, bf16[32,2048]{1,0:T(8,128)(2,1)S(1)} %fusion.83, pred[]{:T(512)S(6)} %compare.3, f32[32,8192]{1,0:T(8,128)S(1)} %fusion.84), kind=kOutput, calls=%fused_computation.21.clone.1 | convolution fusion | flops 1108606976 | bytes 135397376 | tf_op jit(solution)/shard_map/while/body/eval_jaxpr/dot_general | solution.py:27
  1807.7 46.5 %select_add_fusion.4 = f32[2048,8192]{1,0:T(8,128)} fusion(f32[2048,8192]{1,0:T(8,128)} %get-tuple-element.523, pred[]{:T(512)S(6)} %compare.3, bf16[32,8192]{1,0:T(8,128)(2,1)S(1)} %fusion.85, bf16[8,1,32,2048]{3,2,1,0:T(8,128)(2,1)S(1)} %get-tuple-element.545, s32[]{:T(128)S(6)} %min.34), kind=kOutput, calls=%fused_computation.22.clone.1 | convolution fusion | flops 1107296256 | bytes 134873088 | tf_op jit(solution)/shard_map/while/body/eval_jaxpr/dot_general | solution.py:26
  1903.0 46.5 %select_add_fusion.5 = f32[8192,2048]{1,0:T(8,128)} fusion(f32[8192,2048]{1,0:T(8,128)} %get-tuple-element.524, bf16[32,2048]{1,0:T(8,128)(2,1)S(1)} %fusion.83, pred[]{:T(512)S(6)} %compare.3, f32[32,8192]{1,0:T(8,128)S(1)} %fusion.84), kind=kOutput, calls=%fused_computation.21.clone.1 | convolution fusion | flops 1108606976 | bytes 135397376 | tf_op jit(solution)/shard_map/while/body/eval_jaxpr/dot_general | solution.py:27
  1949.5 46.5 %select_add_fusion.4 = f32[2048,8192]{1,0:T(8,128)} fusion(f32[2048,8192]{1,0:T(8,128)} %get-tuple-element.523, pred[]{:T(512)S(6)} %compare.3, bf16[32,8192]{1,0:T(8,128)(2,1)S(1)} %fusion.85, bf16[8,1,32,2048]{3,2,1,0:T(8,128)(2,1)S(1)} %get-tuple-element.545, s32[]{:T(128)S(6)} %min.34), kind=kOutput, calls=%fused_computation.22.clone.1 | convolution fusion | flops 1107296256 | bytes 134873088 | tf_op jit(solution)/shard_map/while/body/eval_jaxpr/dot_general | solution.py:26
  2044.3 46.5 %select_add_fusion.5 = f32[8192,2048]{1,0:T(8,128)} fusion(f32[8192,2048]{1,0:T(8,128)} %get-tuple-element.524, bf16[32,2048]{1,0:T(8,128)(2,1)S(1)} %fusion.83, pred[]{:T(512)S(6)} %compare.3, f32[32,8192]{1,0:T(8,128)S(1)} %fusion.84), kind=kOutput, calls=%fused_computation.21.clone.1 | convolution fusion | flops 1108606976 | bytes 135397376 | tf_op jit(solution)/shard_map/while/body/eval_jaxpr/dot_general | solution.py:27
  2090.8 46.5 %select_add_fusion.4 = f32[2048,8192]{1,0:T(8,128)} fusion(f32[2048,8192]{1,0:T(8,128)} %get-tuple-element.523, pred[]{:T(512)S(6)} %compare.3, bf16[32,8192]{1,0:T(8,128)(2,1)S(1)} %fusion.85, bf16[8,1,32,2048]{3,2,1,0:T(8,128)(2,1)S(1)} %get-tuple-element.545, s32[]{:T(128)S(6)} %min.34), kind=kOutput, calls=%fused_computation.22.clone.1 | convolution fusion | flops 1107296256 | bytes 134873088 | tf_op jit(solution)/shard_map/while/body/eval_jaxpr/dot_general | solution.py:26
  2187.3 46.5 %select_add_fusion.5 = f32[8192,2048]{1,0:T(8,128)} fusion(f32[8192,2048]{1,0:T(8,128)} %get-tuple-element.524, bf16[32,2048]{1,0:T(8,128)(2,1)S(1)} %fusion.83, pred[]{:T(512)S(6)} %compare.3, f32[32,8192]{1,0:T(8,128)S(1)} %fusion.84), kind=kOutput, calls=%fused_computation.21.clone.1 | convolution fusion | flops 1108606976 | bytes 135397376 | tf_op jit(solution)/shard_map/while/body/eval_jaxpr/dot_general | solution.py:27
  2233.8 46.5 %select_add_fusion.4 = f32[2048,8192]{1,0:T(8,128)} fusion(f32[2048,8192]{1,0:T(8,128)} %get-tuple-element.523, pred[]{:T(512)S(6)} %compare.3, bf16[32,8192]{1,0:T(8,128)(2,1)S(1)} %fusion.85, bf16[8,1,32,2048]{3,2,1,0:T(8,128)(2,1)S(1)} %get-tuple-element.545, s32[]{:T(128)S(6)} %min.34), kind=kOutput, calls=%fused_computation.22.clone.1 | convolution fusion | flops 1107296256 | bytes 134873088 | tf_op jit(solution)/shard_map/while/body/eval_jaxpr/dot_general | solution.py:26
  2328.5 46.5 %select_add_fusion.5 = f32[8192,2048]{1,0:T(8,128)} fusion(f32[8192,2048]{1,0:T(8,128)} %get-tuple-element.524, bf16[32,2048]{1,0:T(8,128)(2,1)S(1)} %fusion.83, pred[]{:T(512)S(6)} %compare.3, f32[32,8192]{1,0:T(8,128)S(1)} %fusion.84), kind=kOutput, calls=%fused_computation.21.clone.1 | convolution fusion | flops 1108606976 | bytes 135397376 | tf_op jit(solution)/shard_map/while/body/eval_jaxpr/dot_general | solution.py:27
  2375.0 46.5 %select_add_fusion.4 = f32[2048,8192]{1,0:T(8,128)} fusion(f32[2048,8192]{1,0:T(8,128)} %get-tuple-element.523, pred[]{:T(512)S(6)} %compare.3, bf16[32,8192]{1,0:T(8,128)(2,1)S(1)} %fusion.85, bf16[8,1,32,2048]{3,2,1,0:T(8,128)(2,1)S(1)} %get-tuple-element.545, s32[]{:T(128)S(6)} %min.34), kind=kOutput, calls=%fused_computation.22.clone.1 | convolution fusion | flops 1107296256 | bytes 134873088 | tf_op jit(solution)/shard_map/while/body/eval_jaxpr/dot_general | solution.py:26
  2470.3 46.5 %select_add_fusion.5 = f32[8192,2048]{1,0:T(8,128)} fusion(f32[8192,2048]{1,0:T(8,128)} %get-tuple-element.524, bf16[32,2048]{1,0:T(8,128)(2,1)S(1)} %fusion.83, pred[]{:T(512)S(6)} %compare.3, f32[32,8192]{1,0:T(8,128)S(1)} %fusion.84), kind=kOutput, calls=%fused_computation.21.clone.1 | convolution fusion | flops 1108606976 | bytes 135397376 | tf_op jit(solution)/shard_map/while/body/eval_jaxpr/dot_general | solution.py:27
  2516.8 46.5 %select_add_fusion.4 = f32[2048,8192]{1,0:T(8,128)} fusion(f32[2048,8192]{1,0:T(8,128)} %get-tuple-element.523, pred[]{:T(512)S(6)} %compare.3, bf16[32,8192]{1,0:T(8,128)(2,1)S(1)} %fusion.85, bf16[8,1,32,2048]{3,2,1,0:T(8,128)(2,1)S(1)} %get-tuple-element.545, s32[]{:T(128)S(6)} %min.34), kind=kOutput, calls=%fused_computation.22.clone.1 | convolution fusion | flops 1107296256 | bytes 134873088 | tf_op jit(solution)/shard_map/while/body/eval_jaxpr/dot_general | solution.py:26
  2611.6 46.5 %select_add_fusion.5 = f32[8192,2048]{1,0:T(8,128)} fusion(f32[8192,2048]{1,0:T(8,128)} %get-tuple-element.524, bf16[32,2048]{1,0:T(8,128)(2,1)S(1)} %fusion.83, pred[]{:T(512)S(6)} %compare.3, f32[32,8192]{1,0:T(8,128)S(1)} %fusion.84), kind=kOutput, calls=%fused_computation.21.clone.1 | convolution fusion | flops 1108606976 | bytes 135397376 | tf_op jit(solution)/shard_map/while/body/eval_jaxpr/dot_general | solution.py:27
  2658.1 46.5 %select_add_fusion.4 = f32[2048,8192]{1,0:T(8,128)} fusion(f32[2048,8192]{1,0:T(8,128)} %get-tuple-element.523, pred[]{:T(512)S(6)} %compare.3, bf16[32,8192]{1,0:T(8,128)(2,1)S(1)} %fusion.85, bf16[8,1,32,2048]{3,2,1,0:T(8,128)(2,1)S(1)} %get-tuple-element.545, s32[]{:T(128)S(6)} %min.34), kind=kOutput, calls=%fused_computation.22.clone.1 | convolution fusion | flops 1107296256 | bytes 134873088 | tf_op jit(solution)/shard_map/while/body/eval_jaxpr/dot_general | solution.py:26
  2728.1 728.5 %reduce-scatter.9.cloned.1.call-done = f32[1,2048,4096]{2,1,0:T(8,128)} async-done(((f32[1,2048,8192]{2,1,0:T(8,128)}), f32[1,2048,4096]{2,1,0:T(8,128)}) %reduce-scatter.9.cloned.1.call-update) | async-done | bytes 33554448 | tf_op jit(solution)/shard_map/reduce_scatter | solution.py:124
  3456.6 728.5 %reduce-scatter.11.cloned.1.call-done = f32[1,4096,2048]{2,1,0:T(8,128)} async-done(((f32[1,8192,2048]{2,1,0:T(8,128)}), f32[1,4096,2048]{2,1,0:T(8,128)}) %reduce-scatter.11.cloned.1.call-update) | async-done | bytes 33554448 | tf_op jit(solution)/shard_map/reduce_scatter | solution.py:125
  (223 shorter events, 811.8 us)
Async XLA Ops:
  7.2 18.9 all-gather.7.cloned.1.call-start
  7.9 405.2 %all-gather.11.cloned.1.call-start = ((), (), s32[]{:S(2)}) async-start(), calls=%async_computation.10 | async-start | bytes 50331648 | tf_op jit(solution)/shard_map/all_gather | solution.py:56
  8.6 791.6 %all-gather.13.cloned.1.call-start = ((), (), s32[]{:S(2)}) async-start(), calls=%async_computation.11 | async-start | bytes 50331648 | tf_op jit(solution)/shard_map/all_gather | solution.py:57
  9.4 1185.3 %all-gather.9.cloned.1.call-start = ((), (), s32[]{:S(2)}) async-start(), calls=%async_computation.6 | async-start | bytes 1310720 | tf_op jit(solution)/shard_map/all_gather | solution.py:49
  10.0 2698.8 %reduce-scatter.5.cloned.1.call-start = ((), (), s32[]{:S(2)}) async-start(), calls=%async_computation.5 | async-start | bytes 1310720 | tf_op jit(solution)/shard_map/reduce_scatter | solution.py:86
  830.9 4.4 collective-permute-start
  866.5 4.4 collective-permute-start
  902.1 4.4 collective-permute-start
  937.7 4.4 collective-permute-start
  973.4 4.4 collective-permute-start
  1009.0 4.4 collective-permute-start
  1044.7 4.4 collective-permute-start
  1080.2 4.4 collective-permute-start
  1115.8 4.4 collective-permute-start
  1151.4 4.4 collective-permute-start
  1187.0 4.4 collective-permute-start
  1194.4 1533.7 %reduce-scatter.7.cloned.1.call-start = ((), (), s32[]{:S(2)}) async-start(), calls=%async_computation.7 | async-start | bytes 1310720 | tf_op jit(solution)/shard_map/reduce_scatter | solution.py:127
  1240.7 47.1 %collective-permute-start.1 = (bf16[32,2048]{1,0:T(8,128)(2,1)S(1)}, bf16[32,2048]{1,0:T(8,128)(2,1)S(1)}, u32[]{:S(2)}, u32[]{:S(2)}) collective-permute-start(bf16[32,2048]{1,0:T(8,128)(2,1)S(1)} %fusion.86), channel_id=1, source_target_pairs={{0,3},{1,0},{2,1},{3,2},{4,7},{5,4},{6,5},{7,6}} | collective-permute-start | bytes 393224 | tf_op jit(solution)/shard_map/while/body/eval_jaxpr/ppermute | solution.py:112
  1334.5 95.1 %collective-permute-start.1 = (bf16[32,2048]{1,0:T(8,128)(2,1)S(1)}, bf16[32,2048]{1,0:T(8,128)(2,1)S(1)}, u32[]{:S(2)}, u32[]{:S(2)}) collective-permute-start(bf16[32,2048]{1,0:T(8,128)(2,1)S(1)} %fusion.86), channel_id=1, source_target_pairs={{0,3},{1,0},{2,1},{3,2},{4,7},{5,4},{6,5},{7,6}} | collective-permute-start | bytes 393224 | tf_op jit(solution)/shard_map/while/body/eval_jaxpr/ppermute | solution.py:112
  1476.3 94.6 %collective-permute-start.1 = (bf16[32,2048]{1,0:T(8,128)(2,1)S(1)}, bf16[32,2048]{1,0:T(8,128)(2,1)S(1)}, u32[]{:S(2)}, u32[]{:S(2)}) collective-permute-start(bf16[32,2048]{1,0:T(8,128)(2,1)S(1)} %fusion.86), channel_id=1, source_target_pairs={{0,3},{1,0},{2,1},{3,2},{4,7},{5,4},{6,5},{7,6}} | collective-permute-start | bytes 393224 | tf_op jit(solution)/shard_map/while/body/eval_jaxpr/ppermute | solution.py:112
  1617.5 96.3 %collective-permute-start.1 = (bf16[32,2048]{1,0:T(8,128)(2,1)S(1)}, bf16[32,2048]{1,0:T(8,128)(2,1)S(1)}, u32[]{:S(2)}, u32[]{:S(2)}) collective-permute-start(bf16[32,2048]{1,0:T(8,128)(2,1)S(1)} %fusion.86), channel_id=1, source_target_pairs={{0,3},{1,0},{2,1},{3,2},{4,7},{5,4},{6,5},{7,6}} | collective-permute-start | bytes 393224 | tf_op jit(solution)/shard_map/while/body/eval_jaxpr/ppermute | solution.py:112
  1760.5 94.6 %collective-permute-start.1 = (bf16[32,2048]{1,0:T(8,128)(2,1)S(1)}, bf16[32,2048]{1,0:T(8,128)(2,1)S(1)}, u32[]{:S(2)}, u32[]{:S(2)}) collective-permute-start(bf16[32,2048]{1,0:T(8,128)(2,1)S(1)} %fusion.86), channel_id=1, source_target_pairs={{0,3},{1,0},{2,1},{3,2},{4,7},{5,4},{6,5},{7,6}} | collective-permute-start | bytes 393224 | tf_op jit(solution)/shard_map/while/body/eval_jaxpr/ppermute | solution.py:112
  1901.8 95.1 %collective-permute-start.1 = (bf16[32,2048]{1,0:T(8,128)(2,1)S(1)}, bf16[32,2048]{1,0:T(8,128)(2,1)S(1)}, u32[]{:S(2)}, u32[]{:S(2)}) collective-permute-start(bf16[32,2048]{1,0:T(8,128)(2,1)S(1)} %fusion.86), channel_id=1, source_target_pairs={{0,3},{1,0},{2,1},{3,2},{4,7},{5,4},{6,5},{7,6}} | collective-permute-start | bytes 393224 | tf_op jit(solution)/shard_map/while/body/eval_jaxpr/ppermute | solution.py:112
  2043.6 94.6 %collective-permute-start.1 = (bf16[32,2048]{1,0:T(8,128)(2,1)S(1)}, bf16[32,2048]{1,0:T(8,128)(2,1)S(1)}, u32[]{:S(2)}, u32[]{:S(2)}) collective-permute-start(bf16[32,2048]{1,0:T(8,128)(2,1)S(1)} %fusion.86), channel_id=1, source_target_pairs={{0,3},{1,0},{2,1},{3,2},{4,7},{5,4},{6,5},{7,6}} | collective-permute-start | bytes 393224 | tf_op jit(solution)/shard_map/while/body/eval_jaxpr/ppermute | solution.py:112
  2184.9 96.3 %collective-permute-start.1 = (bf16[32,2048]{1,0:T(8,128)(2,1)S(1)}, bf16[32,2048]{1,0:T(8,128)(2,1)S(1)}, u32[]{:S(2)}, u32[]{:S(2)}) collective-permute-start(bf16[32,2048]{1,0:T(8,128)(2,1)S(1)} %fusion.86), channel_id=1, source_target_pairs={{0,3},{1,0},{2,1},{3,2},{4,7},{5,4},{6,5},{7,6}} | collective-permute-start | bytes 393224 | tf_op jit(solution)/shard_map/while/body/eval_jaxpr/ppermute | solution.py:112
  2327.8 94.6 %collective-permute-start.1 = (bf16[32,2048]{1,0:T(8,128)(2,1)S(1)}, bf16[32,2048]{1,0:T(8,128)(2,1)S(1)}, u32[]{:S(2)}, u32[]{:S(2)}) collective-permute-start(bf16[32,2048]{1,0:T(8,128)(2,1)S(1)} %fusion.86), channel_id=1, source_target_pairs={{0,3},{1,0},{2,1},{3,2},{4,7},{5,4},{6,5},{7,6}} | collective-permute-start | bytes 393224 | tf_op jit(solution)/shard_map/while/body/eval_jaxpr/ppermute | solution.py:112
  2469.1 95.1 %collective-permute-start.1 = (bf16[32,2048]{1,0:T(8,128)(2,1)S(1)}, bf16[32,2048]{1,0:T(8,128)(2,1)S(1)}, u32[]{:S(2)}, u32[]{:S(2)}) collective-permute-start(bf16[32,2048]{1,0:T(8,128)(2,1)S(1)} %fusion.86), channel_id=1, source_target_pairs={{0,3},{1,0},{2,1},{3,2},{4,7},{5,4},{6,5},{7,6}} | collective-permute-start | bytes 393224 | tf_op jit(solution)/shard_map/while/body/eval_jaxpr/ppermute | solution.py:112
  2610.9 94.6 %collective-permute-start.1 = (bf16[32,2048]{1,0:T(8,128)(2,1)S(1)}, bf16[32,2048]{1,0:T(8,128)(2,1)S(1)}, u32[]{:S(2)}, u32[]{:S(2)}) collective-permute-start(bf16[32,2048]{1,0:T(8,128)(2,1)S(1)} %fusion.86), channel_id=1, source_target_pairs={{0,3},{1,0},{2,1},{3,2},{4,7},{5,4},{6,5},{7,6}} | collective-permute-start | bytes 393224 | tf_op jit(solution)/shard_map/while/body/eval_jaxpr/ppermute | solution.py:112
  2707.3 749.3 %reduce-scatter.9.cloned.1.call-start = ((), (), s32[]{:S(2)}) async-start(), calls=%async_computation.8 | async-start | bytes 100663296 | tf_op jit(solution)/shard_map/reduce_scatter | solution.py:124
  2708.0 1477.0 %reduce-scatter.11.cloned.1.call-start = ((), (), s32[]{:S(2)}) async-start(), calls=%async_computation.9 | async-start | bytes 100663296 | tf_op jit(solution)/shard_map/reduce_scatter | solution.py:125
Sparse Core Ops, SparseCore 0:
  9.5 16.5 all-gather.6
  27.6 385.4 all-gather.10
  414.7 385.4 all-gather.12
  801.6 13.7 all-gather.8
  1194.5 18.0 reduce-scatter.4
  2707.4 20.6 reduce-scatter.6
  2730.9 725.6 reduce-scatter.8
  3459.4 725.6 reduce-scatter.10
where the time goes:
time: 4190 us
  waiting for transfers between devices  2290 us (55%)
  matrix products  1780 us (42%)
    reduce_scatter x1, waiting for transfers between devices, device_step(): lax.psum_scatter(jnp.stack(end_state[3]), 'inner', scatter_dimension=1, t...  728 us
    reduce_scatter x1, waiting for transfers between devices, device_step(): lax.psum_scatter(jnp.stack(end_state[2]), 'inner', scatter_dimension=2, t...  728 us
    dot_general x11, matrix products, layer_bwd(): lax.dot_general(act_val, g_out, (((0,), (0,)), ((), ())), preferred_eleme...  488 us
    dot_general x11, matrix products, layer_bwd(): lax.dot_general(h_in, d_pre, (((0,), (0,)), ((), ())), preferred_element_...  488 us
    all_gather x1, waiting for transfers between devices, device_step(): down_full = lax.all_gather(w_down[virt_idx], 'inner', axis=1, tiled=True)  387 us
    all_gather x1, waiting for transfers between devices, device_step(): up_full = lax.all_gather(w_up[virt_idx], 'inner', axis=2, tiled=True)  387 us
    dot_general x11, matrix products, layer_fwd(): branch = jnp.dot(act_val, w_two, preferred_element_type=jnp.float32)  321 us
    dot_general x11, matrix products, layer_bwd(): lax.dot_general(d_pre, w_one, (((1,), (1,)), ((), ())), preferred_element...  167 us
  transfers between devices with their start and end apart: 30, of which 17 were waited for; matrix products, arithmetic and copies ran while one was open for 44% of the time, Pallas kernels for 0%

commit v1 on v0

v1 whole, which is shorter than its diff:
```python
import jax
import jax.numpy as jnp
from jax import lax
from jax.sharding import PartitionSpec as P

F32 = jnp.float32
BF16 = jnp.bfloat16


def gelu_pair(pre_act):
    normal_cdf = 0.5 * (1.0 + lax.erf(pre_act * 0.7071067811865476))
    normal_pdf = jnp.exp(-0.5 * pre_act * pre_act) * 0.3989422804014327
    return pre_act * normal_cdf, normal_cdf + pre_act * normal_pdf


def solution(mesh):
    n_stage = mesh.shape['stage']
    tok_spec = P(('data', 'stage', 'inner'))
    up_spec = P(None, ('data', 'stage'), None, 'inner')
    down_spec = P(None, ('data', 'stage'), 'inner', None)
    fwd_perm = [(i, i + 1) for i in range(n_stage - 1)]
    bwd_perm = [(i, i - 1) for i in range(1, n_stage)]

    def device_step(x_loc, g_loc, w_up, w_down):
        w_one = w_up[0, 0]
        w_two = w_down[0, 0]
        stage = lax.axis_index('stage')
        inner = lax.axis_index('inner')
        d_model = x_loc.shape[2]
        x_all = lax.all_gather(x_loc, ('stage', 'inner'), axis=0, tiled=True)
        g_all = lax.all_gather(g_loc, ('stage', 'inner'), axis=0, tiled=True)
        n_micro, tok = x_all.shape[:2]
        rows = 2 * tok
        n_chunk = n_micro // 2
        x_all = x_all.reshape(n_chunk, rows, d_model)
        g_all = g_all.reshape(n_chunk, rows, d_model)
        first = stage == 0
        last = stage == n_stage - 1
        ticks = n_chunk + n_stage - 1

        recv = jnp.zeros((rows, d_model), BF16)
        h_ticks, a_ticks, d_ticks, y_ticks = [], [], [], []
        for t in range(ticks):
            h_in = jnp.where(first, x_all[min(t, n_chunk - 1)], recv)
            z = jnp.dot(h_in, w_one, preferred_element_type=F32)
            act, slope = gelu_pair(z)
            act = act.astype(BF16)
            part = jnp.dot(act, w_two, preferred_element_type=F32)
            h_out = (h_in.astype(F32) + lax.psum(part, 'inner')).astype(BF16)
            h_ticks.append(h_in)
            a_ticks.append(act)
            d_ticks.append(slope)
            y_ticks.append(h_out)
            if t < ticks - 1:
                recv = lax.ppermute(h_out, 'stage', fwd_perm)
        h_all = jnp.stack(h_ticks)
        a_all = jnp.stack(a_ticks)
        s_all = jnp.stack(d_ticks)

        recv = jnp.zeros((rows, d_model), BF16)
        g_ticks, dz_ticks, hb_ticks, ab_ticks, dx_ticks = [], [], [], [], []
        for t in range(ticks):
            chunk = t - (n_stage - 1 - stage)
            valid = (chunk >= 0) & (chunk < n_chunk)
            slot = jnp.clip(chunk, 0, n_chunk - 1) + stage
            g_in = jnp.where(last, g_all[min(t, n_chunk - 1)], recv)
            g_in = jnp.where(valid, g_in, jnp.zeros_like(g_in))
            h_in = lax.dynamic_index_in_dim(h_all, slot, 0, keepdims=False)
            act = lax.dynamic_index_in_dim(a_all, slot, 0, keepdims=False)
            slope = lax.dynamic_index_in_dim(s_all, slot, 0, keepdims=False)
            err = lax.dot_general(g_in, w_two, (((1,), (1,)), ((), ())), preferred_element_type=F32)
            dz = (err * slope).astype(BF16)
            part = lax.dot_general(dz, w_one, (((1,), (1,)), ((), ())), preferred_element_type=F32)
            g_out = (g_in.astype(F32) + lax.psum(part, 'inner')).astype(BF16)
            g_ticks.append(g_in)
            dz_ticks.append(dz)
            hb_ticks.append(h_in)
            ab_ticks.append(act)
            dx_ticks.append(g_out)
            if t < ticks - 1:
                recv = lax.ppermute(g_out, 'stage', bwd_perm)
        cat = lambda items: jnp.concatenate(items, axis=0)
        contract = (((0,), (0,)), ((), ()))
        dw_up = lax.dot_general(cat(hb_ticks), cat(dz_ticks), contract, preferred_element_type=F32)
        dw_down = lax.dot_general(cat(ab_ticks), cat(g_ticks), contract, preferred_element_type=F32)

        def scatter(items, owner):
            src = jnp.stack(items[n_stage - 1:]).reshape(n_micro, tok, d_model)
            src = jnp.where(owner, src, jnp.zeros_like(src))
            mine = lax.psum_scatter(src, 'stage', scatter_dimension=0, tiled=True)
            return lax.dynamic_slice_in_dim(mine, inner * x_loc.shape[0], x_loc.shape[0], 0)

        return scatter(y_ticks, last), scatter(dx_ticks, first), dw_up[None, None], dw_down[None, None]

    return jax.shard_map(device_step, mesh=mesh, in_specs=(tok_spec, tok_spec, up_spec, down_spec), out_specs=(tok_spec, tok_spec, up_spec, down_spec), check_vma=False)
```

time: 4190 us -> 1300 us (0.31)
  waiting for transfers between devices: 2290 us -> 606 us
  matrix products: 1780 us -> 518 us
    reduce_scatter x4 -> x2, waiting for transfers between devices: 1480 us -> 0.01 us  [scatter(): mine = lax.psum_scatter(src, 'stage', scatter_dimension=0, tiled=True)]
    dot_general x66 -> x46, matrix products: 1780 us -> 518 us  [the longest x11 132 us: device_step(): lax.dot_general(g_in, w_two, (((1,), (1,)), ((), ())), preferred_element_...]
    all_gather x4 -> x2, waiting for transfers between devices: 790 us -> 47 us  [the longest x1 26.7 us: device_step(): x_all = lax.all_gather(x_loc, ('stage', 'inner'), axis=0, tiled=True)]
    psum x0 -> x21, waiting for transfers between devices: none -> 543 us  [the longest x11 306 us: device_step(): h_out = (h_in.astype(F32) + lax.psum(part, 'inner')).astype(BF16)]
    unnamed x2 -> x35, other arithmetic: 0.01 us -> 46.3 us
    unnamed x0 -> x78, local copies, waits for them, and re-layouts: none -> 45.1 us
  transfers between devices with their start and end apart: 30 -> 45, of which waited for: 17 -> 40; matrix products, arithmetic and copies ran while one was open for 44% -> 9% of each run, Pallas kernels for 0% -> 0%
where the time goes in v1:
time: 1300 us; the launch traced here: 1290 us
  waiting for transfers between devices  606 us (47%)
  matrix products  518 us (40%)
  other arithmetic  64.3 us (5%)
  local copies, waits for them, and re-layouts  52 us (4%)
  starting transfers between devices  33.1 us (3%)
  between operations  15.1 us (1%)
    psum x11, waiting for transfers between devices, device_step(): h_out = (h_in.astype(F32) + lax.psum(part, 'inner')).astype(BF16)  306 us
    psum x10, waiting for transfers between devices, device_step(): g_out = (g_in.astype(F32) + lax.psum(part, 'inner')).astype(BF16)  237 us
    dot_general x11, matrix products, device_step(): lax.dot_general(g_in, w_two, (((1,), (1,)), ((), ())), preferred_element_...  132 us
    dot_general x11, matrix products, device_step(): lax.dot_general(dz, w_one, (((1,), (1,)), ((), ())), preferred_element_ty...  131 us
    dot_general x11, matrix products, device_step(): z = jnp.dot(h_in, w_one, preferred_element_type=F32)  110 us
    dot_general x11, matrix products, device_step(): part = jnp.dot(act, w_two, preferred_element_type=F32)  100 us
    unnamed x35, other arithmetic  46.3 us
    unnamed x78, local copies, waits for them, and re-layouts  45.1 us
  transfers between devices with their start and end apart: 45, of which 40 were waited for; matrix products, arithmetic and copies ran while one was open for 9% of the time, Pallas kernels for 0%

profile of v1, /device:TPU:0, one launch (start us, length us, event | category | flops | bytes accessed | tf_op | source)
XLA Modules:
  0.0 1288.7 jit_solution(12097150247639390117)
XLA Ops:
  8.0 26.7 %all-gather.3.cloned.1.call-done = bf16[16,32,2048]{2,1,0:T(8,128)(2,1)} async-done(((bf16[2,32,2048]{2,1,0:T(8,128)(2,1)}), bf16[16,32,2048]{2,1,0:T(8,128)(2,1)}) %all-gather.3.cloned.1.call-update) | async-done | bytes 2097168 | tf_op jit(solution)/shard_map/all_gather | solution.py:30
  51.3 22.9 %all-reduce.23.cloned.1.call-done = f32[64,2048]{1,0:T(8,128)} async-done(((f32[64,2048]{1,0:T(8,128)}), f32[64,2048]{1,0:T(8,128)}) %all-reduce.23.cloned.1.call-update) | async-done | bytes 524304 | tf_op jit(solution)/shard_map/psum | solution.py:49
  99.4 28.0 %all-reduce.25.cloned.1.call-done = f32[64,2048]{1,0:T(8,128)} async-done(((f32[64,2048]{1,0:T(8,128)}), f32[64,2048]{1,0:T(8,128)}) %all-reduce.25.cloned.1.call-update) | async-done | bytes 524304 | tf_op jit(solution)/shard_map/psum | solution.py:49
  151.5 28.0 %all-reduce.27.cloned.1.call-done = f32[64,2048]{1,0:T(8,128)} async-done(((f32[64,2048]{1,0:T(8,128)}), f32[64,2048]{1,0:T(8,128)}) %all-reduce.27.cloned.1.call-update) | async-done | bytes 524304 | tf_op jit(solution)/shard_map/psum | solution.py:49
  202.9 28.0 %all-reduce.29.cloned.1.call-done = f32[64,2048]{1,0:T(8,128)} async-done(((f32[64,2048]{1,0:T(8,128)}), f32[64,2048]{1,0:T(8,128)}) %all-reduce.29.cloned.1.call-update) | async-done | bytes 524304 | tf_op jit(solution)/shard_map/psum | solution.py:49
  256.1 28.0 %all-reduce.31.cloned.1.call-done = f32[64,2048]{1,0:T(8,128)} async-done(((f32[64,2048]{1,0:T(8,128)}), f32[64,2048]{1,0:T(8,128)}) %all-reduce.31.cloned.1.call-update) | async-done | bytes 524304 | tf_op jit(solution)/shard_map/psum | solution.py:49
  309.5 28.0 %all-reduce.33.cloned.1.call-done = f32[64,2048]{1,0:T(8,128)} async-done(((f32[64,2048]{1,0:T(8,128)}), f32[64,2048]{1,0:T(8,128)}) %all-reduce.33.cloned.1.call-update) | async-done | bytes 524304 | tf_op jit(solution)/shard_map/psum | solution.py:49
  362.7 28.0 %all-reduce.35.cloned.1.call-done = f32[64,2048]{1,0:T(8,128)} async-done(((f32[64,2048]{1,0:T(8,128)}), f32[64,2048]{1,0:T(8,128)}) %all-reduce.35.cloned.1.call-update) | async-done | bytes 524304 | tf_op jit(solution)/shard_map/psum | solution.py:49
  415.9 28.0 %all-reduce.37.cloned.1.call-done = f32[64,2048]{1,0:T(8,128)} async-done(((f32[64,2048]{1,0:T(8,128)}), f32[64,2048]{1,0:T(8,128)}) %all-reduce.37.cloned.1.call-update) | async-done | bytes 524304 | tf_op jit(solution)/shard_map/psum | solution.py:49
  469.1 28.0 %all-reduce.39.cloned.1.call-done = f32[64,2048]{1,0:T(8,128)} async-done(((f32[64,2048]{1,0:T(8,128)}), f32[64,2048]{1,0:T(8,128)}) %all-reduce.39.cloned.1.call-update) | async-done | bytes 524304 | tf_op jit(solution)/shard_map/psum | solution.py:49
  523.0 27.4 %all-reduce.41.cloned.1.call-done = f32[64,2048]{1,0:T(8,128)} async-done(((f32[64,2048]{1,0:T(8,128)}), f32[64,2048]{1,0:T(8,128)}) %all-reduce.41.cloned.1.call-update) | async-done | bytes 524304 | tf_op jit(solution)/shard_map/psum | solution.py:49
  554.2 20.4 %all-gather.5.cloned.1.call-done = bf16[16,32,2048]{2,1,0:T(8,128)(2,1)} async-done(((bf16[2,32,2048]{2,1,0:T(8,128)(2,1)}), bf16[16,32,2048]{2,1,0:T(8,128)(2,1)}) %all-gather.5.cloned.1.call-update) | async-done | bytes 2097168 | tf_op jit(solution)/shard_map/all_gather | solution.py:31
  611.5 22.9 %all-reduce.43.cloned.1.call-done = f32[64,2048]{1,0:T(8,128)} async-done(((f32[64,2048]{1,0:T(8,128)}), f32[64,2048]{1,0:T(8,128)}) %all-reduce.43.cloned.1.call-update) | async-done | bytes 524304 | tf_op jit(solution)/shard_map/psum | solution.py:74
  640.7 12.3 constant_dynamic-update-slice_fusion.9
  653.0 12.0 fusion.62
  665.1 25.8 %all-reduce.45.cloned.1.call-done = f32[64,2048]{1,0:T(8,128)} async-done(((f32[64,2048]{1,0:T(8,128)}), f32[64,2048]{1,0:T(8,128)}) %all-reduce.45.cloned.1.call-update) | async-done | bytes 524304 | tf_op jit(solution)/shard_map/psum | solution.py:74
  697.2 12.3 constant_dynamic-update-slice_fusion.8
  709.5 12.0 fusion.60
  722.6 24.8 %all-reduce.47.cloned.1.call-done = f32[64,2048]{1,0:T(8,128)} async-done(((f32[64,2048]{1,0:T(8,128)}), f32[64,2048]{1,0:T(8,128)}) %all-reduce.47.cloned.1.call-update) | async-done | bytes 524304 | tf_op jit(solution)/shard_map/psum | solution.py:74
  753.7 12.0 constant_dynamic-update-slice_fusion.7
  778.6 24.8 %all-reduce.49.cloned.1.call-done = f32[64,2048]{1,0:T(8,128)} async-done(((f32[64,2048]{1,0:T(8,128)}), f32[64,2048]{1,0:T(8,128)}) %all-reduce.49.cloned.1.call-update) | async-done | bytes 524304 | tf_op jit(solution)/shard_map/psum | solution.py:74
  834.4 24.8 %all-reduce.51.cloned.1.call-done = f32[64,2048]{1,0:T(8,128)} async-done(((f32[64,2048]{1,0:T(8,128)}), f32[64,2048]{1,0:T(8,128)}) %all-reduce.51.cloned.1.call-update) | async-done | bytes 524304 | tf_op jit(solution)/shard_map/psum | solution.py:74
  890.2 24.8 %all-reduce.53.cloned.1.call-done = f32[64,2048]{1,0:T(8,128)} async-done(((f32[64,2048]{1,0:T(8,128)}), f32[64,2048]{1,0:T(8,128)}) %all-reduce.53.cloned.1.call-update) | async-done | bytes 524304 | tf_op jit(solution)/shard_map/psum | solution.py:74
  946.1 24.8 %all-reduce.55.cloned.1.call-done = f32[64,2048]{1,0:T(8,128)} async-done(((f32[64,2048]{1,0:T(8,128)}), f32[64,2048]{1,0:T(8,128)}) %all-reduce.55.cloned.1.call-update) | async-done | bytes 524304 | tf_op jit(solution)/shard_map/psum | solution.py:74
  984.7 12.0 constant_dynamic-update-slice_fusion.3
  1011.4 20.9 %all-reduce.57.cloned.1.call-done = f32[64,2048]{1,0:T(8,128)} async-done(((f32[64,2048]{1,0:T(8,128)}), f32[64,2048]{1,0:T(8,128)}) %all-reduce.57.cloned.1.call-update) | async-done | bytes 524304 | tf_op jit(solution)/shard_map/psum | solution.py:74
  1066.3 21.7 %all-reduce.59.cloned.1.call-done = f32[64,2048]{1,0:T(8,128)} async-done(((f32[64,2048]{1,0:T(8,128)}), f32[64,2048]{1,0:T(8,128)}) %all-reduce.59.cloned.1.call-update) | async-done | bytes 524304 | tf_op jit(solution)/shard_map/psum | solution.py:74
  1093.4 12.0 constant_dynamic-update-slice_fusion.1
  1120.9 22.0 %all-reduce.61.cloned.1.call-done = f32[64,2048]{1,0:T(8,128)} async-done(((f32[64,2048]{1,0:T(8,128)}), f32[64,2048]{1,0:T(8,128)}) %all-reduce.61.cloned.1.call-update) | async-done | bytes 524304 | tf_op jit(solution)/shard_map/psum | solution.py:74
  1177.8 31.6 %all-reduce.63.cloned.1.call-done = (f32[64,2048]{1,0:T(8,128)}, f32[64,2048]{1,0:T(8,128)}) async-done(((f32[64,2048]{1,0:T(8,128)}, f32[64,2048]{1,0:T(8,128)}), (f32[64,2048]{1,0:T(8,128)}, f32[64,2048]{1,0:T(8,128)})) %all-reduce.63.cloned.1.call-update) | async-done | bytes 1048592 | tf_op jit(solution)/shard_map/psum | solution.py:49
  1212.3 22.6 %convolution_bitcast_fusion = f32[1,1,4096,2048]{3,2,1,0:T(8,128)} fusion(bf16[704,4096]{1,0:T(8,128)(2,1)} %bitcast_dynamic-update-slice_fusion, bf16[704,2048]{1,0:T(8,128)(2,1)} %get-tuple-element.125), kind=kOutput, calls=%fused_computation | convolution fusion | flops 11811160064 | bytes 42205184 | tf_op jit(solution)/shard_map/dot_general | solution.py:85
  1255.6 22.7 %convolution_bitcast_fusion.1 = f32[1,1,2048,4096]{3,2,1,0:T(8,128)} fusion(bf16[704,2048]{1,0:T(8,128)(2,1)} %bitcast_dynamic-update-slice_fusion.22, bf16[704,4096]{1,0:T(8,128)(2,1)} %get-tuple-element.105), kind=kOutput, calls=%fused_computation.1 | convolution fusion | flops 11811160064 | bytes 42205184 | tf_op jit(solution)/shard_map/dot_general | solution.py:84
  (268 shorter events, 553.4 us)
Async XLA Ops:
  7.2 27.4 %all-gather.3.cloned.1.call-start = ((), (), s32[]{:S(2)}) async-start(), calls=%async_computation.2 | async-start | bytes 2359296 | tf_op jit(solution)/shard_map/all_gather | solution.py:30
  7.9 66.4 %all-reduce.23.cloned.1.call-start = ((), (), s32[]{:S(2)}) async-start(), calls=%async_computation.3 | async-start | bytes 1048576 | tf_op jit(solution)/shard_map/psum | solution.py:49
  51.3 76.1 %all-reduce.25.cloned.1.call-start = ((), (), s32[]{:S(2)}) async-start(), calls=%async_computation.4 | async-start | bytes 1048576 | tf_op jit(solution)/shard_map/psum | solution.py:49
  99.3 80.2 %all-reduce.27.cloned.1.call-start = ((), (), s32[]{:S(2)}) async-start(), calls=%async_computation.5 | async-start | bytes 1048576 | tf_op jit(solution)/shard_map/psum | solution.py:49
  151.4 79.4 %all-reduce.29.cloned.1.call-start = ((), (), s32[]{:S(2)}) async-start(), calls=%async_computation.6 | async-start | bytes 1048576 | tf_op jit(solution)/shard_map/psum | solution.py:49
  202.8 81.3 %all-reduce.31.cloned.1.call-start = ((), (), s32[]{:S(2)}) async-start(), calls=%async_computation.7 | async-start | bytes 1048576 | tf_op jit(solution)/shard_map/psum | solution.py:49
  256.1 81.4 %all-reduce.33.cloned.1.call-start = ((), (), s32[]{:S(2)}) async-start(), calls=%async_computation.8 | async-start | bytes 1048576 | tf_op jit(solution)/shard_map/psum | solution.py:49
  309.4 81.2 %all-reduce.35.cloned.1.call-start = ((), (), s32[]{:S(2)}) async-start(), calls=%async_computation.9 | async-start | bytes 1048576 | tf_op jit(solution)/shard_map/psum | solution.py:49
  362.6 81.3 %all-reduce.37.cloned.1.call-start = ((), (), s32[]{:S(2)}) async-start(), calls=%async_computation.10 | async-start | bytes 1048576 | tf_op jit(solution)/shard_map/psum | solution.py:49
  415.8 81.3 %all-reduce.39.cloned.1.call-start = ((), (), s32[]{:S(2)}) async-start(), calls=%async_computation.11 | async-start | bytes 1048576 | tf_op jit(solution)/shard_map/psum | solution.py:49
  469.1 81.3 %all-reduce.41.cloned.1.call-start = ((), (), s32[]{:S(2)}) async-start(), calls=%async_computation.12 | async-start | bytes 1048576 | tf_op jit(solution)/shard_map/psum | solution.py:49
  522.3 52.3 %all-gather.5.cloned.1.call-start = ((), (), s32[]{:S(2)}) async-start(), calls=%async_computation.14 | async-start | bytes 2359296 | tf_op jit(solution)/shard_map/all_gather | solution.py:31
  522.9 111.5 %all-reduce.43.cloned.1.call-start = ((), (), s32[]{:S(2)}) async-start(), calls=%async_computation.15 | async-start | bytes 1048576 | tf_op jit(solution)/shard_map/psum | solution.py:74
  552.3 25.0 %collective-permute-start.9 = (bf16[64,2048]{1,0:T(8,128)(2,1)S(1)}, bf16[64,2048]{1,0:T(8,128)(2,1)S(1)}, u32[]{:S(2)}, u32[]{:S(2)}) collective-permute-start(bf16[64,2048]{1,0:T(8,128)(2,1)S(1)} %get-tuple-element.21), channel_id=1, source_target_pairs={{0,1},{1,2},{2,3},{4,5},{5,6},{6,7}} | collective-permute-start | bytes 786440 | tf_op jit(solution)/shard_map/ppermute | solution.py:55
  611.4 79.4 %all-reduce.45.cloned.1.call-start = ((), (), s32[]{:S(2)}) async-start(), calls=%async_computation.16 | async-start | bytes 1048576 | tf_op jit(solution)/shard_map/psum | solution.py:74
  635.5 3.4 collective-permute-start.10
  665.0 82.4 %all-reduce.47.cloned.1.call-start = ((), (), s32[]{:S(2)}) async-start(), calls=%async_computation.17 | async-start | bytes 1048576 | tf_op jit(solution)/shard_map/psum | solution.py:74
  692.0 3.4 collective-permute-start.11
  721.5 81.9 %all-reduce.49.cloned.1.call-start = ((), (), s32[]{:S(2)}) async-start(), calls=%async_computation.18 | async-start | bytes 1048576 | tf_op jit(solution)/shard_map/psum | solution.py:74
  777.6 81.6 %all-reduce.51.cloned.1.call-start = ((), (), s32[]{:S(2)}) async-start(), calls=%async_computation.19 | async-start | bytes 1048576 | tf_op jit(solution)/shard_map/psum | solution.py:74
  833.4 81.6 %all-reduce.53.cloned.1.call-start = ((), (), s32[]{:S(2)}) async-start(), calls=%async_computation.20 | async-start | bytes 1048576 | tf_op jit(solution)/shard_map/psum | solution.py:74
  889.2 81.7 %all-reduce.55.cloned.1.call-start = ((), (), s32[]{:S(2)}) async-start(), calls=%async_computation.21 | async-start | bytes 1048576 | tf_op jit(solution)/shard_map/psum | solution.py:74
  945.0 87.2 %all-reduce.57.cloned.1.call-start = ((), (), s32[]{:S(2)}) async-start(), calls=%async_computation.22 | async-start | bytes 1048576 | tf_op jit(solution)/shard_map/psum | solution.py:74
  972.7 11.2 collective-permute-start.16
  1008.5 79.5 %all-reduce.59.cloned.1.call-start = ((), (), s32[]{:S(2)}) async-start(), calls=%async_computation.23 | async-start | bytes 1048576 | tf_op jit(solution)/shard_map/psum | solution.py:74
  1034.0 3.7 collective-permute-start.17
  1062.4 80.6 %all-reduce.61.cloned.1.call-start = ((), (), s32[]{:S(2)}) async-start(), calls=%async_computation.24 | async-start | bytes 1048576 | tf_op jit(solution)/shard_map/psum | solution.py:74
  1089.1 3.4 collective-permute-start.18
  1117.1 92.2 %all-reduce.63.cloned.1.call-start = ((), (), s32[]{:S(2)}) async-start(), calls=%async_computation.26 | async-start | bytes 2097152 | tf_op jit(solution)/shard_map/psum | solution.py:49
  1144.1 3.4 collective-permute-start.19
  1172.1 106.2 %reduce-scatter.5.cloned.1.call-start = ((), (), s32[]{:S(2)}) async-start(), calls=%async_computation.25 | async-start | bytes 2621440 | tf_op jit(solution)/shard_map/reduce_scatter | solution.py:90
  1211.9 68.0 %reduce-scatter.3.cloned.1.call-start = ((), (), s32[]{:S(2)}) async-start(), calls=%async_computation.13 | async-start | bytes 2621440 | tf_op jit(solution)/shard_map/reduce_scatter | solution.py:90
  (41 other events, 578.9 us)
Sparse Core Ops, SparseCore 0:
  9.8 24.7 all-gather.2
  51.4 22.8 all-reduce.22
  99.4 27.8 all-reduce.24
  151.6 27.8 all-reduce.26
  203.0 27.8 all-reduce.28
  256.2 27.8 all-reduce.30
  309.5 27.8 all-reduce.32
  362.7 27.8 all-reduce.34
  416.0 27.8 all-reduce.36
  469.2 27.8 all-reduce.38
  522.5 27.8 all-reduce.40
  552.1 22.4 all-gather.4
  611.6 22.8 all-reduce.42
  665.1 25.6 all-reduce.44
  721.7 25.6 all-reduce.46
  777.7 25.6 all-reduce.48
  833.5 25.6 all-reduce.50
  889.3 25.6 all-reduce.52
  945.2 25.6 all-reduce.54
  1008.6 23.5 all-reduce.56
  1062.5 25.4 all-reduce.58
  1117.3 25.6 all-reduce.60
  1172.2 37.0 all-reduce.62
  1212.1 25.5 reduce-scatter.4
  1245.6 25.4 reduce-scatter.2

commit v2 on v1

v2 whole, which is shorter than its diff:
```python
import functools

import jax
import jax.numpy as jnp
from jax import lax
from jax.experimental import pallas as pl
from jax.experimental.pallas import tpu as pltpu
from jax.sharding import PartitionSpec as P

F32 = jnp.float32
BF16 = jnp.bfloat16
MESH = pl.DeviceIdType.MESH

STAGES = 4
INNER = 2
CHUNKS = 8
BLK = 512
TILE = 256


def gelu_pair(pre_act):
    normal_cdf = 0.5 * (1.0 + lax.erf(pre_act * 0.7071067811865476))
    normal_pdf = jnp.exp(-0.5 * pre_act * pre_act) * 0.3989422804014327
    return pre_act * normal_cdf, normal_cdf + pre_act * normal_pdf


def wait_bytes(ref, sem):
    pltpu.make_async_copy(ref, ref, sem).wait()


def pipeline_kernel(x_ref, g_ref, w1_ref, w2_ref,
                    y_out, dx_out, h_out, g_out, a_out, d_out,
                    wa, wb, hbuf, gbuf, abuf, dbuf, sbuf, pbuf, precv, qrecv, hsend, gsend, ybuf, xbuf,
                    h_sem, g_sem, p_sem, q_sem, blk_send, hs_send, gs_send, home_send, y_sem, x_sem, in_send, w_sem, out_sem):
    stage = lax.axis_index('stage')
    side = lax.axis_index('inner')
    other = 1 - side
    rows = hbuf.shape[2]
    d_model = hbuf.shape[3]
    d_ff = abuf.shape[2]
    tok = 2 * rows
    n_blk = d_model // BLK

    def peer(s, i):
        return {'stage': s, 'inner': i}

    def cols(j):
        return pl.ds(pl.multiple_of(j * BLK, BLK), BLK)

    load_a = pltpu.make_async_copy(w1_ref, wa, w_sem.at[0])
    load_b = pltpu.make_async_copy(w2_ref, wb, w_sem.at[1])
    load_a.start()
    load_b.start()

    barrier = pltpu.get_barrier_semaphore()
    for s in range(STAGES):
        for i in range(INNER):
            @pl.when(jnp.logical_or(stage != s, side != i))
            def _():
                pl.semaphore_signal(barrier, inc=1, device_id=peer(s, i), device_id_type=MESH)
    pl.semaphore_wait(barrier, STAGES * INNER - 1)

    def chunk_of(k):
        return lax.rem(2 * stage + k + CHUNKS - 1, CHUNKS)

    def home_of(c):
        return lax.rem((c + 1) // 2, STAGES)

    def slot_of(c):
        return lax.rem(c + 1, 2)

    def hand_in(src, dst, sem, target, lane):
        for k in range(2):
            c = chunk_of(k)

            @pl.when(stage == target)
            def _():
                pltpu.make_async_copy(src.at[k], dst.at[c, side], sem.at[c, side]).start()

            @pl.when(stage != target)
            def _():
                pltpu.make_async_remote_copy(src.at[k], dst.at[c, side], in_send.at[lane, k, 0], sem.at[c, side],
                                             device_id=peer(target, side), device_id_type=MESH).start()
            pltpu.make_async_remote_copy(src.at[k], dst.at[c, side], in_send.at[lane, k, 1], sem.at[c, side],
                                         device_id=peer(target, other), device_id_type=MESH).start()

    hand_in(x_ref, hbuf, h_sem, 0, 0)
    hand_in(g_ref, gbuf, g_sem, STAGES - 1, 1)

    def up_product(src, c, mode):
        def body(n, carry):
            lhs = src[c].reshape(tok, d_model)
            z = jnp.dot(lhs, wa[:, cols(n)], preferred_element_type=F32)
            if mode == 'back':
                dbuf[c, :, cols(n)] = (z * sbuf[c, :, cols(n)]).astype(BF16)
            else:
                act, slope = gelu_pair(z)
                abuf[c, :, cols(n)] = act.astype(BF16)
                if mode == 'both':
                    dbuf[c, :, cols(n)] = (sbuf[c, :, cols(n)] * slope).astype(BF16)
                else:
                    sbuf[c, :, cols(n)] = slope
            return carry
        lax.fori_loop(0, d_ff // BLK, body, 0, unroll=2)

    def down_product(src, c, slot, reuse, recv, recv_sem):
        def body(j, carry):
            out = pltpu.make_async_remote_copy(pbuf.at[slot, j, other], recv.at[c, j], blk_send.at[slot, j], recv_sem.at[c, j],
                                               device_id=peer(stage, other), device_id_type=MESH)

            @pl.when(reuse)
            def _():
                out.wait_send()
            part = jnp.dot(src[c], wb[:, cols(j)], preferred_element_type=F32)
            pbuf[slot, j] = part.reshape(2, rows, BLK)
            out.start()
            return carry
        lax.fori_loop(0, n_blk, body, 0)

    def drain(slot, recv, recv_sem):
        for j in range(n_blk):
            pltpu.make_async_remote_copy(pbuf.at[slot, j, other], recv.at[0, j], blk_send.at[slot, j], recv_sem.at[0, j],
                                         device_id=peer(stage, other), device_id_type=MESH).wait_send()

    def hand_on(c, slot, recv, recv_sem, res, send, dst, dst_sem, send_sem, target):
        for j in range(n_blk):
            sl = pl.ds(j * BLK, BLK)
            wait_bytes(recv.at[c, j], recv_sem.at[c, j])
            total = res[c, side, :, sl].astype(F32) + (pbuf[slot, j, side] + recv[c, j])
            send[c, :, sl] = total.astype(BF16)
            if target is not None:
                for i in (side, other):
                    pltpu.make_async_remote_copy(send.at[c, :, sl], dst.at[c, side, :, sl], send_sem, dst_sem.at[c, side],
                                                 device_id=peer(target, i), device_id_type=MESH).start()

    def hand_home(c, send, dst, dst_sem, here):
        @pl.when(home_of(c) != here)
        def _():
            pltpu.make_async_remote_copy(send.at[c], dst.at[slot_of(c)], home_send.at[c], dst_sem.at[slot_of(c)],
                                         device_id=peer(home_of(c), side), device_id_type=MESH).start()

    def hand_home_done(send, dst, dst_sem, here):
        for c in range(CHUNKS):
            if (c + 1) // 2 % STAGES != here:
                pltpu.make_async_remote_copy(send.at[c], dst.at[(c + 1) % 2], home_send.at[c], dst_sem.at[(c + 1) % 2],
                                             device_id=peer((c + 1) // 2 % STAGES, side), device_id_type=MESH).wait_send()

    def keep(ref, out, c, lane):
        pltpu.make_async_copy(ref.at[c], out.at[c], out_sem.at[lane]).start()

    def swap_weights():
        n_i = d_model // TILE

        def body(t, carry):
            i = pl.multiple_of(lax.rem(t, n_i) * TILE, TILE)
            j = pl.multiple_of(lax.div(t, n_i) * TILE, TILE)
            up = wa[pl.ds(i, TILE), pl.ds(j, TILE)]
            down = wb[pl.ds(j, TILE), pl.ds(i, TILE)]
            wa[pl.ds(i, TILE), pl.ds(j, TILE)] = down.T
            wb[pl.ds(j, TILE), pl.ds(i, TILE)] = up.T
            return carry
        lax.fori_loop(0, n_i * (d_ff // TILE), body, 0)

    def transpose_up():
        n_i = d_model // TILE

        def body(t, carry):
            i = pl.multiple_of(lax.rem(t, n_i) * TILE, TILE)
            j = pl.multiple_of(lax.div(t, n_i) * TILE, TILE)
            wb[pl.ds(j, TILE), pl.ds(i, TILE)] = wa[pl.ds(i, TILE), pl.ds(j, TILE)].T
            return carry
        lax.fori_loop(0, n_i * (d_ff // TILE), body, 0)

    @pl.when(stage < STAGES - 1)
    def _():
        load_a.wait()

        def fwd(c, carry):
            for i in range(INNER):
                wait_bytes(hbuf.at[c, i], h_sem.at[c, i])
            keep(hbuf, h_out, c, 0)
            up_product(hbuf, c, 'fwd')

            @pl.when(c == 0)
            def _():
                load_b.wait()

            @pl.when(jnp.logical_and(stage == 0, c > 0))
            def _():
                hand_on(c - 1, lax.rem(c + 1, 2), precv, p_sem, hbuf, hsend, hbuf, h_sem, hs_send.at[0], stage + 1)
            keep(abuf, a_out, c, 2)
            down_product(abuf, c, lax.rem(c, 2), c >= 2, precv, p_sem)

            @pl.when(jnp.logical_or(stage != 0, c == CHUNKS - 1))
            def _():
                hand_on(c, lax.rem(c, 2), precv, p_sem, hbuf, hsend, hbuf, h_sem, hs_send.at[0], stage + 1)
            return carry
        lax.fori_loop(0, CHUNKS, fwd, 0)
        swap_weights()

        def bwd(c, carry):
            for i in range(INNER):
                wait_bytes(gbuf.at[c, i], g_sem.at[c, i])
            keep(gbuf, g_out, c, 1)
            up_product(gbuf, c, 'back')

            def pass_back(q):
                @pl.when(stage > 0)
                def _():
                    hand_on(q, lax.rem(q, 2), qrecv, q_sem, gbuf, gsend, gbuf, g_sem, gs_send.at[0], stage - 1)

                @pl.when(stage == 0)
                def _():
                    hand_on(q, lax.rem(q, 2), qrecv, q_sem, gbuf, gsend, None, None, None, None)
                    hand_home(q, gsend, xbuf, x_sem, 0)

            @pl.when(c > 0)
            def _():
                pass_back(c - 1)
            keep(dbuf, d_out, c, 3)
            down_product(dbuf, c, lax.rem(c, 2), c >= 0, qrecv, q_sem)

            @pl.when(c == CHUNKS - 1)
            def _():
                pass_back(c)
            return carry
        lax.fori_loop(0, CHUNKS, bwd, 0)
        for slot in range(2):
            drain(slot, qrecv, q_sem)
        wait_bytes(hbuf, hs_send.at[0])

        @pl.when(stage > 0)
        def _():
            wait_bytes(gbuf, gs_send.at[0])

        @pl.when(stage == 0)
        def _():
            hand_home_done(gsend, xbuf, x_sem, 0)

    @pl.when(stage == STAGES - 1)
    def _():
        load_b.wait()

        half = CHUNKS // 2
        for q in range(2):
            for c in range(half * q, half * q + half):
                for i in range(INNER):
                    wait_bytes(gbuf.at[c, i], g_sem.at[c, i])
                keep(gbuf, g_out, c, 1)

            def err(n, carry):
                lhs = gbuf[half * q:half * q + half].reshape(half * tok, d_model)
                e = lax.dot_general(lhs, wb[cols(n), :], (((1,), (1,)), ((), ())), preferred_element_type=F32)
                sbuf[half * q:half * q + half, :, cols(n)] = e.reshape(half, tok, BLK)
                return carry
            lax.fori_loop(0, d_ff // BLK, err, 0)
        load_a.wait()
        transpose_up()

        def main(c, carry):
            for i in range(INNER):
                wait_bytes(hbuf.at[c, i], h_sem.at[c, i])
            keep(hbuf, h_out, c, 0)
            up_product(hbuf, c, 'both')
            keep(abuf, a_out, c, 2)
            keep(dbuf, d_out, c, 3)
            down_product(dbuf, c, lax.rem(c, 2), c >= 2, qrecv, q_sem)
            hand_on(c, lax.rem(c, 2), qrecv, q_sem, gbuf, gsend, gbuf, g_sem, gs_send.at[0], stage - 1)
            return carry
        lax.fori_loop(0, CHUNKS, main, 0)
        load_b.start()
        load_b.wait()

        def outputs(c, carry):
            down_product(abuf, c, lax.rem(c, 2), c >= 0, precv, p_sem)

            def pass_home(q):
                hand_on(q, lax.rem(q, 2), precv, p_sem, hbuf, hsend, None, None, None, None)
                hand_home(q, hsend, ybuf, y_sem, STAGES - 1)

            @pl.when(c > 0)
            def _():
                pass_home(c - 1)

            @pl.when(c == CHUNKS - 1)
            def _():
                pass_home(c)
            return carry
        lax.fori_loop(0, CHUNKS, outputs, 0)
        for slot in range(2):
            drain(slot, precv, p_sem)
        wait_bytes(gbuf, gs_send.at[0])
        hand_home_done(hsend, ybuf, y_sem, STAGES - 1)

    def come_home(here, send, recv, recv_sem, out, lane):
        for k in range(2):
            @pl.when(stage == here)
            def _():
                pltpu.make_async_copy(send.at[chunk_of(k)], out.at[k], out_sem.at[lane]).start()

            @pl.when(stage != here)
            def _():
                wait_bytes(recv.at[k], recv_sem.at[k])
                pltpu.make_async_copy(recv.at[k], out.at[k], out_sem.at[lane]).start()
    come_home(STAGES - 1, hsend, ybuf, y_sem, y_out, 4)
    come_home(0, gsend, xbuf, x_sem, dx_out, 5)

    for lane, (src, target) in enumerate(((x_ref, 0), (g_ref, STAGES - 1))):
        for k in range(2):
            @pl.when(stage != target)
            def _():
                wait_bytes(src.at[k], in_send.at[lane, k, 0])
            wait_bytes(src.at[k], in_send.at[lane, k, 1])
    for lane, (ref, out) in enumerate(((hbuf, h_out), (gbuf, g_out), (abuf, a_out), (dbuf, d_out), (ybuf, y_out), (xbuf, dx_out))):
        pltpu.make_async_copy(ref, out, out_sem.at[lane]).wait()


def run_pipeline(x_loc, g_loc, w_one, w_two):
    rows, d_model = x_loc.shape[1:]
    d_ff = w_one.shape[1]
    n_blk = d_model // BLK
    tok = 2 * rows
    hbm = pl.BlockSpec(memory_space=pl.ANY)
    out = lambda shape: jax.ShapeDtypeStruct(shape, BF16)
    dma = pltpu.SemaphoreType.DMA
    return pl.pallas_call(
        pipeline_kernel,
        name='pipeline',
        out_shape=(out(x_loc.shape), out(x_loc.shape), out((CHUNKS, 2, rows, d_model)), out((CHUNKS, 2, rows, d_model)),
                   out((CHUNKS, tok, d_ff)), out((CHUNKS, tok, d_ff))),
        in_specs=[hbm] * 4,
        out_specs=(hbm,) * 6,
        scratch_shapes=[
            pltpu.VMEM((d_model, d_ff), BF16),
            pltpu.VMEM((d_ff, d_model), BF16),
            pltpu.VMEM((CHUNKS, 2, rows, d_model), BF16),
            pltpu.VMEM((CHUNKS, 2, rows, d_model), BF16),
            pltpu.VMEM((CHUNKS, tok, d_ff), BF16),
            pltpu.VMEM((CHUNKS, tok, d_ff), BF16),
            pltpu.VMEM((CHUNKS, tok, d_ff), F32),
            pltpu.VMEM((2, n_blk, 2, rows, BLK), F32),
            pltpu.VMEM((CHUNKS, n_blk, rows, BLK), F32),
            pltpu.VMEM((CHUNKS, n_blk, rows, BLK), F32),
            pltpu.VMEM((CHUNKS, rows, d_model), BF16),
            pltpu.VMEM((CHUNKS, rows, d_model), BF16),
            pltpu.VMEM((2, rows, d_model), BF16),
            pltpu.VMEM((2, rows, d_model), BF16),
            dma((CHUNKS, 2)), dma((CHUNKS, 2)), dma((CHUNKS, n_blk)), dma((CHUNKS, n_blk)), dma((2, n_blk)),
            dma((1,)), dma((1,)), dma((CHUNKS,)), dma((2,)), dma((2,)), dma((2, 2, 2)), dma((2,)), dma((6,)),
        ],
        compiler_params=pltpu.CompilerParams(collective_id=0, has_side_effects=True, vmem_limit_bytes=67043328),
    )(x_loc, g_loc, w_one, w_two)


def weight_grad_kernel(h_ref, d_ref, a_ref, g_ref, up_ref, down_ref, *, n_up):
    contract = (((0,), (0,)), ((), ()))

    @pl.when(pl.program_id(0) < n_up)
    def _():
        up_ref[...] = lax.dot_general(h_ref[...], d_ref[...], contract, preferred_element_type=F32)

    @pl.when(pl.program_id(0) >= n_up)
    def _():
        down_ref[...] = lax.dot_general(a_ref[...], g_ref[...], contract, preferred_element_type=F32)


def weight_grads(h, d, a, g):
    tokens, d_model = h.shape
    d_ff = d.shape[1]
    up_rows, down_rows = 256, 512
    n_up, n_down = d_model // up_rows, d_ff // down_rows
    up_idx = lambda i: jnp.minimum(i, n_up - 1)
    down_idx = lambda i: jnp.maximum(i - n_up, 0)
    return pl.pallas_call(
        functools.partial(weight_grad_kernel, n_up=n_up),
        name='weight_grads',
        grid=(n_up + n_down,),
        out_shape=(jax.ShapeDtypeStruct((d_model, d_ff), F32), jax.ShapeDtypeStruct((d_ff, d_model), F32)),
        in_specs=[pl.BlockSpec((tokens, up_rows), lambda i: (0, up_idx(i))),
                  pl.BlockSpec((tokens, d_ff), lambda i: (0, 0)),
                  pl.BlockSpec((tokens, down_rows), lambda i: (0, down_idx(i))),
                  pl.BlockSpec((tokens, d_model), lambda i: (0, 0))],
        out_specs=(pl.BlockSpec((up_rows, d_ff), lambda i: (up_idx(i), 0)),
                   pl.BlockSpec((down_rows, d_model), lambda i: (down_idx(i), 0))),
        compiler_params=pltpu.CompilerParams(vmem_limit_bytes=60 * 1024 * 1024),
    )(h, d, a, g)


def solution(mesh):
    tok_spec = P(('data', 'stage', 'inner'))
    up_spec = P(None, ('data', 'stage'), None, 'inner')
    down_spec = P(None, ('data', 'stage'), 'inner', None)

    def device_step(x_loc, g_loc, w_up, w_down):
        y, dx, h, g, a, d = run_pipeline(x_loc, g_loc, w_up[0, 0], w_down[0, 0])
        flat = lambda v: v.reshape(-1, v.shape[-1])
        dw_up, dw_down = weight_grads(flat(h), flat(d), flat(a), flat(g))
        return y, dx, dw_up[None, None], dw_down[None, None]

    return jax.shard_map(device_step, mesh=mesh, in_specs=(tok_spec, tok_spec, up_spec, down_spec), out_specs=(tok_spec, tok_spec, up_spec, down_spec), check_vma=False)
```

time: 1300 us -> 296 us (0.23)
  waiting for transfers between devices: 606 us -> 0 us
  matrix products: 518 us -> 0 us
  Pallas kernels: 0 us -> 292 us
  other arithmetic: 64.3 us -> 0 us
  local copies, waits for them, and re-layouts: 52 us -> 3.34 us
  starting transfers between devices: 33.1 us -> 0 us
  between operations: 15.1 us -> 0.64 us
    psum x21 -> x0, waiting for transfers between devices: 543 us -> none  [the longest x11 306 us: device_step(): h_out = (h_in.astype(F32) + lax.psum(part, 'inner')).astype(BF16)]
    dot_general x46 -> x0, matrix products: 518 us -> none  [the longest x11 132 us: device_step(): lax.dot_general(g_in, w_two, (((1,), (1,)), ((), ())), preferred_element_...]
    pallas_call x0 -> x2, Pallas kernels: none -> 292 us  [the longest x1 260 us: run_pipeline(): pl.pallas_call(pipeline_kernel, name='pipeline', out_shape=(out(x_loc.sha...]
    all_gather x2 -> x0, waiting for transfers between devices: 47 us -> none  [the longest x1 26.7 us: device_step(): x_all = lax.all_gather(x_loc, ('stage', 'inner'), axis=0, tiled=True)]
    unnamed x35 -> x0, other arithmetic: 46.3 us -> none
    unnamed x78 -> x2, local copies, waits for them, and re-layouts: 45.1 us -> 3.34 us
    ppermute x20 -> x0, starting transfers between devices: 31.8 us -> none  [the longest x10 16.4 us: device_step(): recv = lax.ppermute(h_out, 'stage', fwd_perm)]
    ppermute x20 -> x0, waiting for transfers between devices: 14.1 us -> none  [the longest x10 8.42 us: device_step(): recv = lax.ppermute(h_out, 'stage', fwd_perm)]
  transfers between devices with their start and end apart: 45 -> 0, of which waited for: 40 -> 0; matrix products, arithmetic and copies ran while one was open for 9% -> 0% of each run, Pallas kernels for 0% -> 0%
where the time goes in v2:
time: 296 us
  Pallas kernels  292 us (99%)
  local copies, waits for them, and re-layouts  3.34 us (1%)
    pallas_call x1, Pallas kernels, run_pipeline(): pl.pallas_call(pipeline_kernel, name='pipeline', out_shape=(out(x_loc.sha...  260 us
    pallas_call x1, Pallas kernels, weight_grads(): pl.pallas_call(functools.partial(weight_grad_kernel, n_up=n_up), name='we...  32.2 us

profile of v2, /device:TPU:0, one launch (start us, length us, event | category | flops | bytes accessed | tf_op | source)
XLA Modules:
  0.0 296.1 jit_solution(7265871317622849235)
XLA Ops:
  0.6 259.9 %pipeline.1 = (bf16[2,32,2048]{2,1,0:T(8,128)(2,1)}, bf16[2,32,2048]{2,1,0:T(8,128)(2,1)}, bf16[8,2,32,2048]{3,2,1,0:T(8,128)(2,1)}, bf16[8,2,32,2048]{3,2,1,0:T...) custom-call(bf16[2,32,2048]{2,1,0:T(8,128)(2,1)} %x_ref.1, bf16[2,32,2048]{2,1,0:T(8,128)(2,1)} %g_ref.1, ...), custom_call_target="tpu_custom_call" | custom-call | tf_op jit(solution)/shard_map/pipeline/pallas_call | solution.py:326
  260.6 32.2 %weight_grads.1 = (f32[2048,4096]{1,0:T(8,128)}, f32[4096,2048]{1,0:T(8,128)}) custom-call(bf16[512,2048]{1,0:T(8,128)(2,1)} %bitcast.12, bf16[512,4096]{1,0:T(8,128)(2,1)} %bitcast.11, bf16[512,4096]{1,0:T(8,128)(2,1)} %bitcast.10, bf16[512,2048]{1,0:T(8,128)(2,1)} %bitcast.13), custom_call_target="tpu_custom_call" | custom-call | tf_op jit(solution)/shard_map/weight_grads/pallas_call | solution.py:374
  292.8 1.7 copy.10
  294.5 1.7 copy.11

commit v3 on v1

v3 whole, which is shorter than its diff:
```python
import functools

import jax
import jax.numpy as jnp
from jax import lax
from jax.experimental import pallas as pl
from jax.experimental.pallas import tpu as pltpu
from jax.sharding import PartitionSpec as P

F32 = jnp.float32
BF16 = jnp.bfloat16
MESH = pl.DeviceIdType.MESH

STAGES = 4
INNER = 2
UNITS = 8
SLOTS = 4
BLK = 512
TILE = 256
FWD, BWD = 0, 1
NT = (((1,), (1,)), ((), ()))

F1, F2, FR, B1, B2, BR, T1, T2, SW, PR, YL, WA, WB, XS = range(1, 15)
PLAN = (
    ((WA, 0, 1), (F1, 0, 1), (WB, 0, 1), (F2, 0, 1), (F1, 1, 2), (FR, 0, 1), (F2, 1, 1), (F2, 2, 1),
     (FR, 1, 1), (F1, 3, 1), (F1, 4, 2), (FR, 2, 1), (F2, 3, 1), (F1, 6, 2), (F2, 4, 1), (FR, 3, 2),
     (F2, 5, 2), (FR, 5, 2), (F2, 7, 1), (SW, 0, 1), (FR, 7, 1), (B1, 0, 2), (B2, 0, 1), (B2, 1, 1),
     (BR, 0, 1), (B1, 2, 2), (B2, 2, 2), (B1, 4, 2), (BR, 1, 3), (B2, 4, 2), (B1, 6, 2), (B2, 6, 2),
     (BR, 4, 4)),
    ((WA, 0, 1), (WB, 0, 1), (F1, 0, 1), (F2, 0, 1), (FR, 0, 1), (F1, 1, 1), (F2, 1, 1), (F1, 2, 1),
     (FR, 1, 1), (F2, 2, 1), (FR, 2, 1), (F1, 3, 2), (F2, 3, 1), (F2, 4, 1), (FR, 3, 1), (F1, 5, 2),
     (F2, 5, 1), (FR, 4, 2), (F2, 6, 1), (F1, 7, 1), (F2, 7, 1), (FR, 6, 2), (SW, 0, 1), (B1, 0, 2),
     (B2, 0, 1), (B2, 1, 1), (BR, 0, 2), (B1, 2, 2), (B2, 2, 2), (BR, 2, 2), (B1, 4, 2), (B2, 4, 1),
     (B2, 5, 1), (B1, 6, 2), (BR, 4, 1), (B2, 6, 1), (BR, 5, 1), (B2, 7, 1), (BR, 6, 2)),
    ((WA, 0, 1), (XS, 0, 1), (WB, 0, 1), (F1, 0, 1), (F2, 0, 1), (FR, 0, 1), (F1, 1, 1), (F2, 1, 1),
     (F1, 2, 1), (FR, 1, 1), (F2, 2, 1), (FR, 2, 1), (F1, 3, 1), (F2, 3, 1), (F1, 4, 2), (F2, 4, 1),
     (F2, 5, 1), (FR, 3, 2), (T1, 0, 2), (FR, 5, 1), (T2, 0, 2), (F1, 6, 2), (F2, 6, 2), (BR, 0, 2),
     (T1, 2, 2), (FR, 6, 2), (T2, 2, 2), (BR, 2, 2), (T1, 4, 2), (T2, 4, 2), (T1, 6, 2), (BR, 4, 2),
     (T2, 6, 2), (BR, 6, 2)),
    ((WB, 0, 1), (XS, 0, 1), (PR, 0, 1), (F1, 0, 1), (B2, 0, 1), (F1, 1, 1), (BR, 0, 1), (B2, 1, 1),
     (BR, 1, 1), (F1, 2, 1), (B2, 2, 1), (BR, 2, 1), (F1, 3, 1), (F1, 4, 1), (B2, 3, 1), (F1, 5, 1),
     (BR, 3, 1), (B2, 4, 2), (F1, 6, 2), (BR, 4, 2), (B2, 6, 2), (BR, 6, 2), (YL, 0, 1), (F2, 0, 2),
     (FR, 0, 1), (F2, 2, 1), (FR, 1, 2), (F2, 3, 1), (F2, 4, 1), (FR, 3, 2), (F2, 5, 2), (FR, 5, 1),
     (F2, 7, 1), (FR, 6, 2)),
)


PACK = 1024


def plan_words():
    rows = [[op + 16 * unit + 128 * (count - 1) for op, unit, count in row] for row in PLAN]
    steps = -(-max(len(row) for row in rows) // 3) * 3
    rows = [row + [0] * (steps - len(row)) for row in rows]
    return steps, [[row[t] + PACK * row[t + 1] + PACK * PACK * row[t + 2] for t in range(0, steps, 3)] for row in rows]


def gelu_pair(pre_act):
    normal_cdf = 0.5 * (1.0 + lax.erf(pre_act * 0.7071067811865476))
    normal_pdf = jnp.exp(-0.5 * pre_act * pre_act) * 0.3989422804014327
    return pre_act * normal_cdf, normal_cdf + pre_act * normal_pdf


def wait_bytes(ref, sem):
    pltpu.make_async_copy(ref, ref, sem).wait()


def pipeline_kernel(x_ref, g_ref, w1_ref, w2_ref,
                    y_out, dx_out, h_out, g_out, a_out, d_out,
                    wa, wb, flow, act, slope, part, recv, send, home,
                    flow_sem, recv_sem, part_send, flow_send, home_send, home_sem, in_send, w_sem, out_sem):
    stage = lax.axis_index('stage')
    side = lax.axis_index('inner')
    other = 1 - side
    rows, d_model = flow.shape[3:]
    tok, d_ff = act.shape[2:]
    n_blk = d_model // BLK

    def peer(s, i):
        return {'stage': s, 'inner': i}

    load_a = pltpu.make_async_copy(w1_ref, wa, w_sem.at[0])
    load_b = pltpu.make_async_copy(w2_ref, wb, w_sem.at[1])

    @pl.when(stage < STAGES - 1)
    def _():
        load_a.start()
    load_b.start()

    @pl.when(stage == STAGES - 1)
    def _():
        load_a.start()

    barrier = pltpu.get_barrier_semaphore()
    for s in range(STAGES):
        for i in range(INNER):
            @pl.when(jnp.logical_or(stage != s, side != i))
            def _():
                pl.semaphore_signal(barrier, inc=1, device_id=peer(s, i), device_id_type=MESH)
    pl.semaphore_wait(barrier, STAGES * INNER - 1)

    def unit_of(k):
        return lax.rem(2 * stage + k + UNITS - 1, UNITS)

    def home_of(u):
        return lax.rem((u + 1) // 2, STAGES)

    def slot_of(u):
        return lax.rem(u + 1, 2)

    def hand_in(kind, src, target, k, lane):
        u = unit_of(k)
        if lane == 0:
            @pl.when(stage == target)
            def _():
                pltpu.make_async_copy(src.at[k], flow.at[kind, u, side], flow_sem.at[kind, u, side]).start()

            @pl.when(stage != target)
            def _():
                pltpu.make_async_remote_copy(src.at[k], flow.at[kind, u, side], in_send.at[kind, k, 0], flow_sem.at[kind, u, side],
                                             device_id=peer(target, side), device_id_type=MESH).start()
        else:
            pltpu.make_async_remote_copy(src.at[k], flow.at[kind, u, side], in_send.at[kind, k, 1], flow_sem.at[kind, u, side],
                                         device_id=peer(target, other), device_id_type=MESH).start()

    for k in (1, 0):
        hand_in(FWD, x_ref, 0, k, 0)

        @pl.when(stage < 2)
        def _():
            hand_in(FWD, x_ref, 0, k, 1)
    for k in (1, 0):
        for lane in range(2):
            hand_in(BWD, g_ref, STAGES - 1, k, lane)

    steps, plan = plan_words()
    words = [jnp.where(stage == 0, a, jnp.where(stage == 1, b, jnp.where(stage == 2, c, d))) for a, b, c, d in zip(*plan)]

    def keep(ref, out, u, lane):
        pltpu.make_async_copy(ref, out.at[u], out_sem.at[lane]).start()

    def blocks(width, group, fn):
        def body(t, carry):
            fn([pl.ds(pl.multiple_of((t * group + k) * BLK, BLK), BLK) for k in range(group)])
            return carry
        lax.fori_loop(0, width // BLK // group, body, 0)

    def arrived(kind, u, count):
        for i in range(count):
            for half in range(INNER):
                wait_bytes(flow.at[kind, u + i, half], flow_sem.at[kind, u + i, half])

    def up_product(u, count):
        arrived(FWD, u, count)
        units = pl.ds(u, count)

        def fn(slices):
            lhs = flow[FWD, units].reshape(count * tok, d_model)
            for sl in slices:
                z = jnp.dot(lhs, wa[:, sl], preferred_element_type=F32).reshape(count, tok, BLK)
                value, grad = gelu_pair(z)
                act[FWD, units, :, sl] = value.astype(BF16)
                act[BWD, units, :, sl] = (slope[units, :, sl] * grad).astype(BF16)
                slope[units, :, sl] = grad
        blocks(d_ff, 4, fn)
        for i in range(count):
            keep(flow.at[FWD, u + i], h_out, u + i, 0)
            keep(act.at[FWD, u + i], a_out, u + i, 2)

            @pl.when(stage == STAGES - 1)
            def _():
                keep(act.at[BWD, u + i], d_out, u + i, 3)

    def back_product(u, count, swapped):
        arrived(BWD, u, count)
        units = pl.ds(u, count)

        def fn(slices):
            lhs = flow[BWD, units].reshape(count * tok, d_model)
            for sl in slices:
                if swapped:
                    e = jnp.dot(lhs, wa[:, sl], preferred_element_type=F32)
                else:
                    e = lax.dot_general(lhs, wb[sl, :], NT, preferred_element_type=F32)
                act[BWD, units, :, sl] = (e.reshape(count, tok, BLK) * slope[units, :, sl]).astype(BF16)
        blocks(d_ff, 4, fn)
        for i in range(count):
            keep(flow.at[BWD, u + i], g_out, u + i, 1)
            keep(act.at[BWD, u + i], d_out, u + i, 3)

    def part_copy(kind, u, j):
        slot = lax.rem(u, SLOTS)
        return pltpu.make_async_remote_copy(part.at[kind, slot, j, other], recv.at[kind, u, j], part_send.at[kind, slot, j],
                                            recv_sem.at[kind, u, j], device_id=peer(stage, other), device_id_type=MESH)

    def down_product(kind, u, count, straight):
        for i in range(count):
            @pl.when(u + i >= SLOTS)
            def _():
                for j in range(n_blk):
                    part_copy(kind, u + i - SLOTS, j).wait_send()

        def body(t, carry):
            lhs = act[kind, pl.ds(u, count)].reshape(count * tok, d_ff)
            for k in range(2):
                j = t * 2 + k
                sl = pl.ds(pl.multiple_of(j * BLK, BLK), BLK)
                if straight:
                    p = jnp.dot(lhs, wb[:, sl], preferred_element_type=F32)
                else:
                    p = lax.dot_general(lhs, wa[sl, :], NT, preferred_element_type=F32)
                p = p.reshape(count, INNER, rows, BLK)
                for i in range(count):
                    part[kind, lax.rem(u + i, SLOTS), j] = p[i]
            for k in range(2):
                for i in range(count):
                    part_copy(kind, u + i, t * 2 + k).start()
            return carry
        lax.fori_loop(0, n_blk // 2, body, 0)

    def hand_on(kind, first, count):
        target = stage + 1 if kind == FWD else stage - 1
        inside = stage < STAGES - 1 if kind == FWD else stage > 0
        out = STAGES - 1 if kind == FWD else 0

        def body(i, carry):
            u = first + i
            slot = lax.rem(u, SLOTS)
            for j in range(n_blk):
                sl = pl.ds(j * BLK, BLK)
                wait_bytes(recv.at[kind, u, j], recv_sem.at[kind, u, j])
                total = flow[kind, u, side, :, sl].astype(F32) + (part[kind, slot, j, side] + recv[kind, u, j])
                send[kind, u, :, sl] = total.astype(BF16)

                @pl.when(inside)
                def _():
                    for half in (side, other):
                        pltpu.make_async_remote_copy(send.at[kind, u, :, sl], flow.at[kind, u, side, :, sl], flow_send.at[kind],
                                                     flow_sem.at[kind, u, side], device_id=peer(target, half), device_id_type=MESH).start()

            @pl.when(jnp.logical_and(jnp.logical_not(inside), home_of(u) != out))
            def _():
                pltpu.make_async_remote_copy(send.at[kind, u], home.at[kind, slot_of(u)], home_send.at[kind, u],
                                             home_sem.at[kind, slot_of(u)], device_id=peer(home_of(u), side), device_id_type=MESH).start()
            return carry
        lax.fori_loop(0, count, body, 0)

    def swap_weights():
        n_i = d_model // TILE

        def body(t, carry):
            i = pl.multiple_of(lax.rem(t, n_i) * TILE, TILE)
            j = pl.multiple_of(lax.div(t, n_i) * TILE, TILE)
            up = wa[pl.ds(i, TILE), pl.ds(j, TILE)]
            down = wb[pl.ds(j, TILE), pl.ds(i, TILE)]
            wa[pl.ds(i, TILE), pl.ds(j, TILE)] = down.T
            wb[pl.ds(j, TILE), pl.ds(i, TILE)] = up.T
            return carry
        lax.fori_loop(0, n_i * (d_ff // TILE), body, 0)

    def prepare_last():
        half = UNITS // 2

        def quarter(q, carry):
            for i in range(half):
                arrived(BWD, q * half + i, 1)
                keep(flow.at[BWD, q * half + i], g_out, q * half + i, 1)
            units = pl.ds(q * half, half)

            def fn(slices):
                lhs = flow[BWD, units].reshape(half * tok, d_model)
                for sl in slices:
                    e = lax.dot_general(lhs, wb[sl, :], NT, preferred_element_type=F32)
                    slope[units, :, sl] = e.reshape(half, tok, BLK)
            blocks(d_ff, 1, fn)
            return carry
        lax.fori_loop(0, 2, quarter, 0)
        load_a.wait()
        n_i = d_model // TILE

        def body(t, carry):
            i = pl.multiple_of(lax.rem(t, n_i) * TILE, TILE)
            j = pl.multiple_of(lax.div(t, n_i) * TILE, TILE)
            wb[pl.ds(j, TILE), pl.ds(i, TILE)] = wa[pl.ds(i, TILE), pl.ds(j, TILE)].T
            return carry
        lax.fori_loop(0, n_i * (d_ff // TILE), body, 0)

    def step(t, carry):
        group, place = lax.div(t, 3), lax.rem(t, 3)
        word = words[0]
        for i, w in enumerate(words[1:], 1):
            word = jnp.where(group == i, w, word)
        code = lax.rem(lax.div(word, jnp.where(place == 0, 1, jnp.where(place == 1, PACK, PACK * PACK))), PACK)
        op = lax.rem(code, 16)
        u = lax.rem(lax.div(code, 16), UNITS)
        count = lax.div(code, 128) + 1

        def on(*want):
            hit = op == want[0]
            if len(want) > 1:
                hit = jnp.logical_and(hit, count == want[1])
            return pl.when(hit)

        for n in (1, 2):
            @on(F1, n)
            def _():
                up_product(u, n)

        for n in (1, 2):
            @pl.when(jnp.logical_and(jnp.logical_or(op == F2, op == B2), count == n))
            def _():
                down_product(jnp.where(op == F2, FWD, BWD), u, n, True)

        @on(FR)
        def _():
            hand_on(FWD, u, count)

        @on(BR)
        def _():
            hand_on(BWD, u, count)

        @on(B1)
        def _():
            back_product(u, 2, True)

        @on(T1)
        def _():
            back_product(u, 2, False)

        @on(T2)
        def _():
            down_product(BWD, u, 2, False)

        @on(SW)
        def _():
            swap_weights()

        @on(PR)
        def _():
            prepare_last()

        @on(YL)
        def _():
            load_b.start()
            load_b.wait()

        @on(WA)
        def _():
            load_a.wait()

        @on(WB)
        def _():
            load_b.wait()

        @on(XS)
        def _():
            for k in (1, 0):
                hand_in(FWD, x_ref, 0, k, 1)
        return carry
    lax.fori_loop(0, steps, step, 0)

    for kind, here, out in ((FWD, STAGES - 1, y_out), (BWD, 0, dx_out)):
        for k in range(2):
            @pl.when(stage == here)
            def _():
                pltpu.make_async_copy(send.at[kind, unit_of(k)], out.at[k], out_sem.at[4 + kind]).start()

            @pl.when(stage != here)
            def _():
                wait_bytes(home.at[kind, k], home_sem.at[kind, k])
                pltpu.make_async_copy(home.at[kind, k], out.at[k], out_sem.at[4 + kind]).start()

    for kind in (FWD, BWD):
        for u in range(UNITS - SLOTS, UNITS):
            for j in range(n_blk):
                @pl.when(stage < STAGES)
                def _():
                    part_copy(kind, u, j).wait_send()
    for kind, target, src in ((FWD, 0, x_ref), (BWD, STAGES - 1, g_ref)):
        last = STAGES - 1 - target
        for k in range(2):
            @pl.when(stage != target)
            def _():
                wait_bytes(src.at[k], in_send.at[kind, k, 0])
            wait_bytes(src.at[k], in_send.at[kind, k, 1])

        @pl.when(stage != last)
        def _():
            wait_bytes(flow.at[kind], flow_send.at[kind])

        @pl.when(stage == last)
        def _():
            for u in range(UNITS):
                if (u + 1) // 2 % STAGES != last:
                    wait_bytes(send.at[kind, u], home_send.at[kind, u])
    for lane, (ref, out) in enumerate(((flow.at[FWD], h_out), (flow.at[BWD], g_out), (act.at[FWD], a_out), (act.at[BWD], d_out),
                                       (home.at[FWD], y_out), (home.at[BWD], dx_out))):
        pltpu.make_async_copy(ref, out, out_sem.at[lane]).wait()


def run_pipeline(x_loc, g_loc, w_one, w_two):
    rows, d_model = x_loc.shape[1:]
    d_ff = w_one.shape[1]
    n_blk = d_model // BLK
    tok = INNER * rows
    hbm = pl.BlockSpec(memory_space=pl.ANY)
    out = lambda *shape: jax.ShapeDtypeStruct(shape, BF16)
    dma = lambda *shape: pltpu.SemaphoreType.DMA(shape)
    return pl.pallas_call(
        pipeline_kernel,
        name='pipeline',
        out_shape=(out(*x_loc.shape), out(*x_loc.shape), out(UNITS, INNER, rows, d_model), out(UNITS, INNER, rows, d_model),
                   out(UNITS, tok, d_ff), out(UNITS, tok, d_ff)),
        in_specs=[hbm] * 4,
        out_specs=(hbm,) * 6,
        scratch_shapes=[
            pltpu.VMEM((d_model, d_ff), BF16),
            pltpu.VMEM((d_ff, d_model), BF16),
            pltpu.VMEM((2, UNITS, INNER, rows, d_model), BF16),
            pltpu.VMEM((2, UNITS, tok, d_ff), BF16),
            pltpu.VMEM((UNITS, tok, d_ff), F32),
            pltpu.VMEM((2, SLOTS, n_blk, INNER, rows, BLK), F32),
            pltpu.VMEM((2, UNITS, n_blk, rows, BLK), F32),
            pltpu.VMEM((2, UNITS, rows, d_model), BF16),
            pltpu.VMEM((2, 2, rows, d_model), BF16),
            dma(2, UNITS, INNER), dma(2, UNITS, n_blk), dma(2, SLOTS, n_blk), dma(2), dma(2, UNITS), dma(2, 2), dma(2, 2, 2), dma(2), dma(6),
        ],
        compiler_params=pltpu.CompilerParams(collective_id=0, has_side_effects=True, vmem_limit_bytes=67043328),
    )(x_loc, g_loc, w_one, w_two)


def weight_grad_kernel(h_ref, d_ref, a_ref, g_ref, y_ref, x_ref, up_ref, down_ref, y_out, x_out, *, n_up):
    contract = (((0,), (0,)), ((), ()))

    @pl.when(pl.program_id(0) == 0)
    def _():
        y_out[...] = y_ref[...]
        x_out[...] = x_ref[...]

    @pl.when(pl.program_id(0) < n_up)
    def _():
        up_ref[...] = lax.dot_general(h_ref[...], d_ref[...], contract, preferred_element_type=F32)

    @pl.when(pl.program_id(0) >= n_up)
    def _():
        down_ref[...] = lax.dot_general(a_ref[...], g_ref[...], contract, preferred_element_type=F32)


def weight_grads(h, d, a, g, y, dx):
    tokens, d_model = h.shape
    d_ff = d.shape[1]
    up_rows, down_rows = 256, 512
    n_up, n_down = d_model // up_rows, d_ff // down_rows
    up_idx = lambda i: jnp.minimum(i, n_up - 1)
    down_idx = lambda i: jnp.maximum(i - n_up, 0)
    whole = pl.BlockSpec(y.shape, lambda i: (0, 0, 0))
    return pl.pallas_call(
        functools.partial(weight_grad_kernel, n_up=n_up),
        name='weight_grads',
        grid=(n_up + n_down,),
        out_shape=(jax.ShapeDtypeStruct((d_model, d_ff), F32), jax.ShapeDtypeStruct((d_ff, d_model), F32),
                   jax.ShapeDtypeStruct(y.shape, BF16), jax.ShapeDtypeStruct(y.shape, BF16)),
        in_specs=[pl.BlockSpec((tokens, up_rows), lambda i: (0, up_idx(i))),
                  pl.BlockSpec((tokens, d_ff), lambda i: (0, 0)),
                  pl.BlockSpec((tokens, down_rows), lambda i: (0, down_idx(i))),
                  pl.BlockSpec((tokens, d_model), lambda i: (0, 0)), whole, whole],
        out_specs=(pl.BlockSpec((up_rows, d_ff), lambda i: (up_idx(i), 0)),
                   pl.BlockSpec((down_rows, d_model), lambda i: (down_idx(i), 0)), whole, whole),
        compiler_params=pltpu.CompilerParams(vmem_limit_bytes=60 * 1024 * 1024),
    )(h, d, a, g, y, dx)


def solution(mesh):
    tok_spec = P(('data', 'stage', 'inner'))
    up_spec = P(None, ('data', 'stage'), None, 'inner')
    down_spec = P(None, ('data', 'stage'), 'inner', None)

    def device_step(x_loc, g_loc, w_up, w_down):
        y, dx, h, g, a, d = run_pipeline(x_loc, g_loc, w_up[0, 0], w_down[0, 0])
        flat = lambda v: v.reshape(-1, v.shape[-1])
        dw_up, dw_down, y, dx = weight_grads(flat(h), flat(d), flat(a), flat(g), y, dx)
        return y, dx, dw_up[None, None], dw_down[None, None]

    return jax.shard_map(device_step, mesh=mesh, in_specs=(tok_spec, tok_spec, up_spec, down_spec), out_specs=(tok_spec, tok_spec, up_spec, down_spec), check_vma=False)
```

time: 1300 us -> 246 us (0.19)
  waiting for transfers between devices: 606 us -> 0 us
  matrix products: 518 us -> 0 us
  Pallas kernels: 0 us -> 245 us
  other arithmetic: 64.3 us -> 0 us
  local copies, waits for them, and re-layouts: 52 us -> 0 us
  starting transfers between devices: 33.1 us -> 0 us
  between operations: 15.1 us -> 0.64 us
    psum x21 -> x0, waiting for transfers between devices: 543 us -> none  [the longest x11 306 us: device_step(): h_out = (h_in.astype(F32) + lax.psum(part, 'inner')).astype(BF16)]
    dot_general x46 -> x0, matrix products: 518 us -> none  [the longest x11 132 us: device_step(): lax.dot_general(g_in, w_two, (((1,), (1,)), ((), ())), preferred_element_...]
    pallas_call x0 -> x2, Pallas kernels: none -> 245 us  [the longest x1 213 us: run_pipeline(): pl.pallas_call(pipeline_kernel, name='pipeline', out_shape=(out(*x_loc.sh...]
    all_gather x2 -> x0, waiting for transfers between devices: 47 us -> none  [the longest x1 26.7 us: device_step(): x_all = lax.all_gather(x_loc, ('stage', 'inner'), axis=0, tiled=True)]
    unnamed x35 -> x0, other arithmetic: 46.3 us -> none
    unnamed x78 -> x0, local copies, waits for them, and re-layouts: 45.1 us -> none
    ppermute x20 -> x0, starting transfers between devices: 31.8 us -> none  [the longest x10 16.4 us: device_step(): recv = lax.ppermute(h_out, 'stage', fwd_perm)]
    ppermute x20 -> x0, waiting for transfers between devices: 14.1 us -> none  [the longest x10 8.42 us: device_step(): recv = lax.ppermute(h_out, 'stage', fwd_perm)]
  transfers between devices with their start and end apart: 45 -> 0, of which waited for: 40 -> 0; matrix products, arithmetic and copies ran while one was open for 9% -> 0% of each run, Pallas kernels for 0% -> 0%
where the time goes in v3:
time: 246 us
  Pallas kernels  245 us (100%)
    pallas_call x1, Pallas kernels, run_pipeline(): pl.pallas_call(pipeline_kernel, name='pipeline', out_shape=(out(*x_loc.sh...  213 us
    pallas_call x1, Pallas kernels, weight_grads(): pl.pallas_call(functools.partial(weight_grad_kernel, n_up=n_up), name='we...  32.2 us

profile of v3, /device:TPU:0, one launch (start us, length us, event | category | flops | bytes accessed | tf_op | source)
XLA Modules:
  0.0 245.9 jit_solution(1108652918550324554)
XLA Ops:
  0.6 213.0 %pipeline.1 = (bf16[2,32,2048]{2,1,0:T(8,128)(2,1)}, bf16[2,32,2048]{2,1,0:T(8,128)(2,1)}, bf16[8,2,32,2048]{3,2,1,0:T(8,128)(2,1)}, bf16[8,2,32,2048]{3,2,1,0:T...) custom-call(bf16[2,32,2048]{2,1,0:T(8,128)(2,1)} %x_ref.1, bf16[2,32,2048]{2,1,0:T(8,128)(2,1)} %g_ref.1, ...), custom_call_target="tpu_custom_call" | custom-call | tf_op jit(solution)/shard_map/pipeline/pallas_call | solution.py:409
  213.7 32.2 %weight_grads.1 = (f32[2048,4096]{1,0:T(8,128)}, f32[4096,2048]{1,0:T(8,128)}, bf16[2,32,2048]{2,1,0:T(8,128)(2,1)}, bf16[2,32,2048]{2,1,0:T(8,128)(2,1)}) custom-call(bf16[512,2048]{1,0:T(8,128)(2,1)} %bitcast.12, bf16[512,4096]{1,0:T(8,128)(2,1)} %bitcast.11, bf16[512,4096]{1,0:T(8,128)(2,1)} %bitcast.10, bf16[512,2048]{1,0:T(8,128)(2,1)} %bitcast.13, ...), custom_call_target="tpu_custom_call" | custom-call | tf_op jit(solution)/shard_map/weight_grads/pallas_call | solution.py:457

commit v4 on v3

--- a/solution.py
+++ b/solution.py
@@ -22,30 +22,31 @@
 
 F1, F2, FR, B1, B2, BR, T1, T2, SW, PR, YL, WA, WB, XS = range(1, 15)
 PLAN = (
-    ((WA, 0, 1), (F1, 0, 1), (WB, 0, 1), (F2, 0, 1), (F1, 1, 2), (FR, 0, 1), (F2, 1, 1), (F2, 2, 1),
-     (FR, 1, 1), (F1, 3, 1), (F1, 4, 2), (FR, 2, 1), (F2, 3, 1), (F1, 6, 2), (F2, 4, 1), (FR, 3, 2),
-     (F2, 5, 2), (FR, 5, 2), (F2, 7, 1), (SW, 0, 1), (FR, 7, 1), (B1, 0, 2), (B2, 0, 1), (B2, 1, 1),
-     (BR, 0, 1), (B1, 2, 2), (B2, 2, 2), (B1, 4, 2), (BR, 1, 3), (B2, 4, 2), (B1, 6, 2), (B2, 6, 2),
-     (BR, 4, 4)),
-    ((WA, 0, 1), (WB, 0, 1), (F1, 0, 1), (F2, 0, 1), (FR, 0, 1), (F1, 1, 1), (F2, 1, 1), (F1, 2, 1),
-     (FR, 1, 1), (F2, 2, 1), (FR, 2, 1), (F1, 3, 2), (F2, 3, 1), (F2, 4, 1), (FR, 3, 1), (F1, 5, 2),
-     (F2, 5, 1), (FR, 4, 2), (F2, 6, 1), (F1, 7, 1), (F2, 7, 1), (FR, 6, 2), (SW, 0, 1), (B1, 0, 2),
-     (B2, 0, 1), (B2, 1, 1), (BR, 0, 2), (B1, 2, 2), (B2, 2, 2), (BR, 2, 2), (B1, 4, 2), (B2, 4, 1),
-     (B2, 5, 1), (B1, 6, 2), (BR, 4, 1), (B2, 6, 1), (BR, 5, 1), (B2, 7, 1), (BR, 6, 2)),
-    ((WA, 0, 1), (XS, 0, 1), (WB, 0, 1), (F1, 0, 1), (F2, 0, 1), (FR, 0, 1), (F1, 1, 1), (F2, 1, 1),
-     (F1, 2, 1), (FR, 1, 1), (F2, 2, 1), (FR, 2, 1), (F1, 3, 1), (F2, 3, 1), (F1, 4, 2), (F2, 4, 1),
-     (F2, 5, 1), (FR, 3, 2), (T1, 0, 2), (FR, 5, 1), (T2, 0, 2), (F1, 6, 2), (F2, 6, 2), (BR, 0, 2),
-     (T1, 2, 2), (FR, 6, 2), (T2, 2, 2), (BR, 2, 2), (T1, 4, 2), (T2, 4, 2), (T1, 6, 2), (BR, 4, 2),
-     (T2, 6, 2), (BR, 6, 2)),
+    ((WA, 0, 1), (F1, 0, 1), (WB, 0, 1), (XS, 0, 1), (F1, 1, 2), (F2, 0, 1), (F2, 1, 1), (FR, 0, 1),
+     (F2, 2, 1), (FR, 1, 1), (F1, 3, 2), (FR, 2, 1), (F2, 3, 1), (FR, 3, 1), (F1, 5, 1), (F2, 4, 2),
+     (F1, 6, 2), (FR, 4, 2), (F2, 6, 1), (F2, 7, 1), (FR, 6, 2), (SW, 0, 1), (B1, 0, 2), (B2, 0, 1),
+     (B2, 1, 1), (BR, 0, 1), (B1, 2, 2), (B2, 2, 2), (BR, 1, 3), (B1, 4, 2), (B2, 4, 2), (B1, 6, 2),
+     (B2, 6, 2), (BR, 4, 4)),
+    ((WA, 0, 1), (WB, 0, 1), (F1, 0, 1), (F2, 0, 1), (F1, 1, 2), (F2, 1, 2), (FR, 0, 3), (F1, 3, 1),
+     (F2, 3, 1), (FR, 3, 1), (F1, 4, 2), (F2, 4, 1), (F2, 5, 1), (F1, 6, 2), (FR, 4, 2), (F2, 6, 1),
+     (F2, 7, 1), (FR, 6, 2), (SW, 0, 1), (B1, 0, 2), (B2, 0, 2), (BR, 0, 2), (B1, 2, 2), (B2, 2, 1),
+     (B2, 3, 1), (BR, 2, 2), (B1, 4, 1), (B2, 4, 1), (B1, 5, 1), (B2, 5, 1), (B1, 6, 1), (B1, 7, 1),
+     (BR, 4, 1), (B2, 6, 1), (BR, 5, 1), (B2, 7, 1), (BR, 6, 2)),
+    ((WA, 0, 1), (WB, 0, 1), (XS, 0, 1), (F1, 0, 1), (F2, 0, 1), (F1, 1, 2), (FR, 0, 1), (F2, 1, 1),
+     (F2, 2, 1), (FR, 1, 1), (F1, 3, 1), (FR, 2, 1), (F2, 3, 1), (FR, 3, 1), (F1, 4, 2), (F2, 4, 2),
+     (F1, 6, 2), (F2, 6, 1), (T1, 0, 2), (FR, 4, 2), (T2, 0, 2), (F2, 7, 1), (BR, 0, 2), (FR, 6, 2),
+     (T1, 2, 2), (T2, 2, 2), (T1, 4, 2), (BR, 2, 2), (T2, 4, 2), (T1, 6, 2), (BR, 4, 1), (T2, 6, 2),
+     (BR, 5, 3)),
     ((WB, 0, 1), (XS, 0, 1), (PR, 0, 1), (F1, 0, 1), (B2, 0, 1), (F1, 1, 1), (BR, 0, 1), (B2, 1, 1),
-     (BR, 1, 1), (F1, 2, 1), (B2, 2, 1), (BR, 2, 1), (F1, 3, 1), (F1, 4, 1), (B2, 3, 1), (F1, 5, 1),
-     (BR, 3, 1), (B2, 4, 2), (F1, 6, 2), (BR, 4, 2), (B2, 6, 2), (BR, 6, 2), (YL, 0, 1), (F2, 0, 2),
-     (FR, 0, 1), (F2, 2, 1), (FR, 1, 2), (F2, 3, 1), (F2, 4, 1), (FR, 3, 2), (F2, 5, 2), (FR, 5, 1),
-     (F2, 7, 1), (FR, 6, 2)),
+     (BR, 1, 1), (F1, 2, 1), (B2, 2, 1), (F1, 3, 1), (B2, 3, 1), (F1, 4, 2), (BR, 2, 2), (B2, 4, 1),
+     (B2, 5, 1), (BR, 4, 2), (F1, 6, 2), (B2, 6, 1), (B2, 7, 1), (BR, 6, 2), (YL, 0, 1), (F2, 0, 1),
+     (F2, 1, 1), (FR, 0, 2), (F2, 2, 2), (FR, 2, 2), (F2, 4, 2), (FR, 4, 2), (F2, 6, 2), (FR, 6, 2)),
 )
 
 
 PACK = 1024
+UP_GROUP = 8
+DOWN_GROUP = 2
 
 
 def plan_words():
@@ -123,13 +124,13 @@
             pltpu.make_async_remote_copy(src.at[k], flow.at[kind, u, side], in_send.at[kind, k, 1], flow_sem.at[kind, u, side],
                                          device_id=peer(target, other), device_id_type=MESH).start()
 
-    for k in (1, 0):
+    for k in range(2):
         hand_in(FWD, x_ref, 0, k, 0)
 
-        @pl.when(stage < 2)
+        @pl.when(jnp.logical_or(stage == 1, jnp.logical_and(stage == 0, k == 1)))
         def _():
             hand_in(FWD, x_ref, 0, k, 1)
-    for k in (1, 0):
+    for k in range(2):
         for lane in range(2):
             hand_in(BWD, g_ref, STAGES - 1, k, lane)
 
@@ -145,78 +146,106 @@
             return carry
         lax.fori_loop(0, width // BLK // group, body, 0)
 
-    def arrived(kind, u, count):
-        for i in range(count):
-            for half in range(INNER):
-                wait_bytes(flow.at[kind, u + i, half], flow_sem.at[kind, u + i, half])
-
-    def up_product(u, count):
-        arrived(FWD, u, count)
-        units = pl.ds(u, count)
+    def arrived(kind, u):
+        for half in range(INNER):
+            wait_bytes(flow.at[kind, u, half], flow_sem.at[kind, u, half])
+
+    def both_arrived(kind, u, v):
+        arrived(kind, u)
+
+        @pl.when(v != u)
+        def _():
+            arrived(kind, v)
+
+    def pair(ref, kind, u, v):
+        width = ref.shape[-1]
+        return jnp.concatenate([ref[kind, u].reshape(tok, width), ref[kind, v].reshape(tok, width)], axis=0)
+
+    def kept(u, v, fn):
+        fn(u)
+
+        @pl.when(v != u)
+        def _():
+            fn(v)
+
+    def up_product(u, v):
+        both_arrived(FWD, u, v)
 
         def fn(slices):
-            lhs = flow[FWD, units].reshape(count * tok, d_model)
+            lhs = pair(flow, FWD, u, v)
             for sl in slices:
-                z = jnp.dot(lhs, wa[:, sl], preferred_element_type=F32).reshape(count, tok, BLK)
+                z = jnp.dot(lhs, wa[:, sl], preferred_element_type=F32)
                 value, grad = gelu_pair(z)
-                act[FWD, units, :, sl] = value.astype(BF16)
-                act[BWD, units, :, sl] = (slope[units, :, sl] * grad).astype(BF16)
-                slope[units, :, sl] = grad
-        blocks(d_ff, 4, fn)
-        for i in range(count):
-            keep(flow.at[FWD, u + i], h_out, u + i, 0)
-            keep(act.at[FWD, u + i], a_out, u + i, 2)
+                value = value.astype(BF16)
+                first, second = slope[u, :, sl], slope[v, :, sl]
+                act[BWD, u, :, sl] = (first * grad[:tok]).astype(BF16)
+                act[BWD, v, :, sl] = (second * grad[tok:]).astype(BF16)
+                slope[u, :, sl] = grad[:tok]
+                slope[v, :, sl] = grad[tok:]
+                act[FWD, u, :, sl] = value[:tok]
+                act[FWD, v, :, sl] = value[tok:]
+        blocks(d_ff, UP_GROUP, fn)
+
+        def out(w):
+            keep(flow.at[FWD, w], h_out, w, 0)
+            keep(act.at[FWD, w], a_out, w, 2)
 
             @pl.when(stage == STAGES - 1)
             def _():
-                keep(act.at[BWD, u + i], d_out, u + i, 3)
-
-    def back_product(u, count, swapped):
-        arrived(BWD, u, count)
-        units = pl.ds(u, count)
+                keep(act.at[BWD, w], d_out, w, 3)
+        kept(u, v, out)
+
+    def back_product(u, v, swapped):
+        both_arrived(BWD, u, v)
 
         def fn(slices):
-            lhs = flow[BWD, units].reshape(count * tok, d_model)
+            lhs = pair(flow, BWD, u, v)
             for sl in slices:
                 if swapped:
                     e = jnp.dot(lhs, wa[:, sl], preferred_element_type=F32)
                 else:
                     e = lax.dot_general(lhs, wb[sl, :], NT, preferred_element_type=F32)
-                act[BWD, units, :, sl] = (e.reshape(count, tok, BLK) * slope[units, :, sl]).astype(BF16)
-        blocks(d_ff, 4, fn)
-        for i in range(count):
-            keep(flow.at[BWD, u + i], g_out, u + i, 1)
-            keep(act.at[BWD, u + i], d_out, u + i, 3)
+                act[BWD, u, :, sl] = (e[:tok] * slope[u, :, sl]).astype(BF16)
+                act[BWD, v, :, sl] = (e[tok:] * slope[v, :, sl]).astype(BF16)
+        blocks(d_ff, UP_GROUP, fn)
+
+        def out(w):
+            keep(flow.at[BWD, w], g_out, w, 1)
+            keep(act.at[BWD, w], d_out, w, 3)
+        kept(u, v, out)
 
     def part_copy(kind, u, j):
         slot = lax.rem(u, SLOTS)
         return pltpu.make_async_remote_copy(part.at[kind, slot, j, other], recv.at[kind, u, j], part_send.at[kind, slot, j],
                                             recv_sem.at[kind, u, j], device_id=peer(stage, other), device_id_type=MESH)
 
-    def down_product(kind, u, count, straight):
-        for i in range(count):
-            @pl.when(u + i >= SLOTS)
+    def down_product(kind, u, v, straight):
+        def free(w):
+            @pl.when(w >= SLOTS)
             def _():
                 for j in range(n_blk):
-                    part_copy(kind, u + i - SLOTS, j).wait_send()
+                    part_copy(kind, w - SLOTS, j).wait_send()
+        kept(u, v, free)
 
         def body(t, carry):
-            lhs = act[kind, pl.ds(u, count)].reshape(count * tok, d_ff)
-            for k in range(2):
-                j = t * 2 + k
+            lhs = pair(act, kind, u, v)
+            for k in range(DOWN_GROUP):
+                j = t * DOWN_GROUP + k
                 sl = pl.ds(pl.multiple_of(j * BLK, BLK), BLK)
                 if straight:
                     p = jnp.dot(lhs, wb[:, sl], preferred_element_type=F32)
                 else:
                     p = lax.dot_general(lhs, wa[sl, :], NT, preferred_element_type=F32)
-                p = p.reshape(count, INNER, rows, BLK)
-                for i in range(count):
-                    part[kind, lax.rem(u + i, SLOTS), j] = p[i]
-            for k in range(2):
-                for i in range(count):
-                    part_copy(kind, u + i, t * 2 + k).start()
+                p = p.reshape(2, INNER, rows, BLK)
+                part[kind, lax.rem(u, SLOTS), j] = p[0]
+                part[kind, lax.rem(v, SLOTS), j] = p[1]
+
+            def go(w):
+                for k in range(DOWN_GROUP):
+                    part_copy(kind, w, t * DOWN_GROUP + k).start()
+            kept(u, v, go)
             return carry
-        lax.fori_loop(0, n_blk // 2, body, 0)
+        lax.fori_loop(0, n_blk // DOWN_GROUP, body, 0)
 
     def hand_on(kind, first, count):
         target = stage + 1 if kind == FWD else stage - 1
@@ -263,7 +292,7 @@
 
         def quarter(q, carry):
             for i in range(half):
-                arrived(BWD, q * half + i, 1)
+                arrived(BWD, q * half + i)
                 keep(flow.at[BWD, q * half + i], g_out, q * half + i, 1)
             units = pl.ds(q * half, half)
 
@@ -295,21 +324,18 @@
         u = lax.rem(lax.div(code, 16), UNITS)
         count = lax.div(code, 128) + 1
 
-        def on(*want):
-            hit = op == want[0]
-            if len(want) > 1:
-                hit = jnp.logical_and(hit, count == want[1])
-            return pl.when(hit)
-
-        for n in (1, 2):
-            @on(F1, n)
-            def _():
-                up_product(u, n)
-
-        for n in (1, 2):
-            @pl.when(jnp.logical_and(jnp.logical_or(op == F2, op == B2), count == n))
-            def _():
-                down_product(jnp.where(op == F2, FWD, BWD), u, n, True)
+        def on(want):
+            return pl.when(op == want)
+
+        v = jnp.minimum(u + count - 1, UNITS - 1)
+
+        @on(F1)
+        def _():
+            up_product(u, v)
+
+        @pl.when(jnp.logical_or(op == F2, op == B2))
+        def _():
+            down_product(jnp.where(op == F2, FWD, BWD), u, v, True)
 
         @on(FR)
         def _():
@@ -321,15 +347,15 @@
 
         @on(B1)
         def _():
-            back_product(u, 2, True)
+            back_product(u, v, True)
 
         @on(T1)
         def _():
-            back_product(u, 2, False)
+            back_product(u, v, False)
 
         @on(T2)
         def _():
-            down_product(BWD, u, 2, False)
+            down_product(BWD, u, v, False)
 
         @on(SW)
         def _():
@@ -354,8 +380,10 @@
 
         @on(XS)
         def _():
-            for k in (1, 0):
-                hand_in(FWD, x_ref, 0, k, 1)
+            for k in range(2):
+                @pl.when(jnp.logical_or(stage > 1, k == 0))
+                def _():
+                    hand_in(FWD, x_ref, 0, k, 1)
         return carry
     lax.fori_loop(0, steps, step, 0)
 
@@ -373,9 +401,7 @@
     for kind in (FWD, BWD):
         for u in range(UNITS - SLOTS, UNITS):
             for j in range(n_blk):
-                @pl.when(stage < STAGES)
-                def _():
-                    part_copy(kind, u, j).wait_send()
+                part_copy(kind, u, j).wait_send()
     for kind, target, src in ((FWD, 0, x_ref), (BWD, STAGES - 1, g_ref)):
         last = STAGES - 1 - target
         for k in range(2):
@@ -429,43 +455,82 @@
     )(x_loc, g_loc, w_one, w_two)
 
 
-def weight_grad_kernel(h_ref, d_ref, a_ref, g_ref, y_ref, x_ref, up_ref, down_ref, y_out, x_out, *, n_up):
-    contract = (((0,), (0,)), ((), ()))
-
-    @pl.when(pl.program_id(0) == 0)
-    def _():
-        y_out[...] = y_ref[...]
-        x_out[...] = x_ref[...]
-
-    @pl.when(pl.program_id(0) < n_up)
-    def _():
-        up_ref[...] = lax.dot_general(h_ref[...], d_ref[...], contract, preferred_element_type=F32)
-
-    @pl.when(pl.program_id(0) >= n_up)
-    def _():
-        down_ref[...] = lax.dot_general(a_ref[...], g_ref[...], contract, preferred_element_type=F32)
+GRAD_ROWS, GRAD_COLS = 1024, 2048
+
+
+def weight_grad_kernel(h_ref, d_ref, a_ref, g_ref, y_ref, x_ref, up_ref, down_ref, y_out, x_out,
+                       h, d, a, g, home, stage, in_sem, home_sem, out_sem):
+    tokens, d_model = h.shape
+    d_ff = d.shape[1]
+    n_down, n_up = d_ff // GRAD_ROWS, d_model // GRAD_ROWS
+    n_col = d_ff // GRAD_COLS
+
+    loads = [(g_ref, g)] + [(a_ref.at[:, pl.ds(t * GRAD_ROWS, GRAD_ROWS)], a.at[:, pl.ds(t * GRAD_ROWS, GRAD_ROWS)]) for t in range(n_down)] + [(h_ref, h), (d_ref, d)]
+    loads = [pltpu.make_async_copy(src, dst, in_sem.at[t]) for t, (src, dst) in enumerate(loads)]
+    homes = [pltpu.make_async_copy(src, home.at[t], home_sem.at[t]) for t, src in enumerate((y_ref, x_ref))]
+    for copy in loads + homes:
+        copy.start()
+    loads[0].wait()
+
+    def block(t, src, first, other, second, out, pieces=1):
+        slot = lax.rem(t, 2)
+        size = GRAD_ROWS // pieces
+        for p in range(pieces):
+            rows = pl.ds(pl.multiple_of(first + p * size, size), size)
+            cols = pl.ds(pl.multiple_of(second, GRAD_COLS), GRAD_COLS)
+            stage[slot, pl.ds(p * size, size)] = lax.dot_general(src[:, rows], other[:, cols], (((0,), (0,)), ((), ())), preferred_element_type=F32)
+            pltpu.make_async_copy(stage.at[slot, pl.ds(p * size, size)], out.at[rows, cols], out_sem.at[slot]).start()
+
+    def freed(slot):
+        pltpu.make_async_copy(stage.at[slot], stage.at[slot], out_sem.at[slot]).wait()
+
+    def down(t, carry):
+        pltpu.make_async_copy(a_ref.at[:, pl.ds(0, GRAD_ROWS)], a.at[:, pl.ds(0, GRAD_ROWS)], in_sem.at[1 + t]).wait()
+
+        @pl.when(t >= 2)
+        def _():
+            freed(lax.rem(t, 2))
+        block(t, a, t * GRAD_ROWS, g, 0, down_ref)
+        return carry
+    lax.fori_loop(0, n_down, down, 0)
+    loads[1 + n_down].wait()
+    loads[2 + n_down].wait()
+    for copy, (src, dst) in zip(homes, ((home.at[0], y_out), (home.at[1], x_out))):
+        copy.wait()
+    backs = [pltpu.make_async_copy(home.at[t], dst, home_sem.at[t]) for t, dst in enumerate((y_out, x_out))]
+    for copy in backs:
+        copy.start()
+
+    def up(t, carry):
+        freed(lax.rem(t, 2))
+        block(t, h, lax.div(t, n_col) * GRAD_ROWS, d, lax.rem(t, n_col) * GRAD_COLS, up_ref)
+        return carry
+    n_blocks = n_up * n_col
+    lax.fori_loop(0, n_blocks - 1, up, 0)
+    freed((n_blocks - 1) % 2)
+    block(n_blocks - 1, h, (n_up - 1) * GRAD_ROWS, d, (n_col - 1) * GRAD_COLS, up_ref, 4)
+    for slot in range(2):
+        freed(slot)
+    for copy in backs:
+        copy.wait()
 
 
 def weight_grads(h, d, a, g, y, dx):
     tokens, d_model = h.shape
     d_ff = d.shape[1]
-    up_rows, down_rows = 256, 512
-    n_up, n_down = d_model // up_rows, d_ff // down_rows
-    up_idx = lambda i: jnp.minimum(i, n_up - 1)
-    down_idx = lambda i: jnp.maximum(i - n_up, 0)
-    whole = pl.BlockSpec(y.shape, lambda i: (0, 0, 0))
+    n_in = 3 + d_ff // GRAD_ROWS
+    hbm = pl.BlockSpec(memory_space=pl.ANY)
+    dma = lambda *shape: pltpu.SemaphoreType.DMA(shape)
+    like = lambda v: pltpu.VMEM(v.shape, v.dtype)
     return pl.pallas_call(
-        functools.partial(weight_grad_kernel, n_up=n_up),
+        weight_grad_kernel,
         name='weight_grads',
-        grid=(n_up + n_down,),
         out_shape=(jax.ShapeDtypeStruct((d_model, d_ff), F32), jax.ShapeDtypeStruct((d_ff, d_model), F32),
                    jax.ShapeDtypeStruct(y.shape, BF16), jax.ShapeDtypeStruct(y.shape, BF16)),
-        in_specs=[pl.BlockSpec((tokens, up_rows), lambda i: (0, up_idx(i))),
-                  pl.BlockSpec((tokens, d_ff), lambda i: (0, 0)),
-                  pl.BlockSpec((tokens, down_rows), lambda i: (0, down_idx(i))),
-                  pl.BlockSpec((tokens, d_model), lambda i: (0, 0)), whole, whole],
-        out_specs=(pl.BlockSpec((up_rows, d_ff), lambda i: (up_idx(i), 0)),
-                   pl.BlockSpec((down_rows, d_model), lambda i: (down_idx(i), 0)), whole, whole),
+        in_specs=[hbm] * 6,
+        out_specs=(hbm,) * 4,
+        scratch_shapes=[like(h), like(d), like(a), like(g), pltpu.VMEM((2,) + y.shape, BF16), pltpu.VMEM((2, GRAD_ROWS, GRAD_COLS), F32),
+                        dma(n_in), dma(2), dma(2)],
         compiler_params=pltpu.CompilerParams(vmem_limit_bytes=60 * 1024 * 1024),
     )(h, d, a, g, y, dx)
 

time: 246 us -> 233 us (0.947)
  Pallas kernels: 245 us -> 232 us
    pallas_call x1, Pallas kernels: 213 us -> 205 us  [run_pipeline(): pl.pallas_call(pipeline_kernel, name='pipeline', out_shape=(out(*x_loc.sh...]
    pallas_call x1, Pallas kernels: 32.2 us -> 27.4 us  [weight_grads(): pl.pallas_call(weight_grad_kernel, name='weight_grads', out_shape=(jax.Sh...]
where the time goes in v4:
time: 233 us
  Pallas kernels  232 us (100%)
    pallas_call x1, Pallas kernels, run_pipeline(): pl.pallas_call(pipeline_kernel, name='pipeline', out_shape=(out(*x_loc.sh...  205 us
    pallas_call x1, Pallas kernels, weight_grads(): pl.pallas_call(weight_grad_kernel, name='weight_grads', out_shape=(jax.Sh...  27.4 us

profile of v4, /device:TPU:0, one launch (start us, length us, event | category | flops | bytes accessed | tf_op | source)
XLA Modules:
  0.0 233.2 jit_solution(18077610646504466977)
XLA Ops:
  0.6 205.0 %pipeline.1 = (bf16[2,32,2048]{2,1,0:T(8,128)(2,1)}, bf16[2,32,2048]{2,1,0:T(8,128)(2,1)}, bf16[8,2,32,2048]{3,2,1,0:T(8,128)(2,1)}, bf16[8,2,32,2048]{3,2,1,0:T...) custom-call(bf16[2,32,2048]{2,1,0:T(8,128)(2,1)} %x_ref.1, bf16[2,32,2048]{2,1,0:T(8,128)(2,1)} %g_ref.1, ...), custom_call_target="tpu_custom_call" | custom-call | tf_op jit(solution)/shard_map/pipeline/pallas_call | solution.py:435
  205.6 27.4 %weight_grads.1 = (f32[2048,4096]{1,0:T(8,128)}, f32[4096,2048]{1,0:T(8,128)}, bf16[2,32,2048]{2,1,0:T(8,128)(2,1)}, bf16[2,32,2048]{2,1,0:T(8,128)(2,1)}) custom-call(bf16[512,2048]{1,0:T(8,128)(2,1)} %bitcast.12, bf16[512,4096]{1,0:T(8,128)(2,1)} %bitcast.11, bf16[512,4096]{1,0:T(8,128)(2,1)} %bitcast.10, bf16[512,2048]{1,0:T(8,128)(2,1)} %bitcast.13, ...), custom_call_target="tpu_custom_call" | custom-call | tf_op jit(solution)/shard_map/weight_grads/pallas_call | solution.py:525
